TPU v7x, 32 devices: a whole 2x2x4 slice. The times are simulated.
32 devices in a mesh: dp: 16 (over z, x, core), tensor: 2 (over y).
Axes of the slice: x: 2, y: 2, z: 4, core: 2. Of those that a mesh axis runs over, the one named last changes fastest.
Arguments:
- pixels: bfloat16 [32, 256, 768], P('dp'), may hold values from 0.03 to 4.4
- lengths: int32 [32], P('dp'), may hold values from 1 to 256, 6144 in all
- patch_ids: int32 [32, 256], P('dp'), may hold values from 0 to 783, as said below
- gsd_values: int32 [32], P('dp'), may hold values from 30 to 300
- embed_w: bfloat16 [768, 1024], replicated, may hold values from -0.21875 to 0.21875
- embed_bias: float32 [1024], replicated, may hold values from -1.5 to 1.5
- norm_gain: float32 [2, 1024], replicated, may hold values from 0.25 to 1.75
- norm_bias: float32 [2, 1024], replicated, may hold values from -1.5 to 1.5
- qkv_w: bfloat16 [3, 1024, 1024], P(None, None, 'tensor'), may hold values from -0.1875 to 0.1875
- qv_bias: float32 [2, 1024], P(None, 'tensor'), may hold values from -1.5 to 1.5
- out_w: bfloat16 [1024, 1024], P('tensor'), may hold values from -1 to 1
- out_bias: float32 [1024], replicated, may hold values from -1.5 to 1.5
- up_w: bfloat16 [1024, 4096], P(None, 'tensor'), may hold values from -0.1875 to 0.1875
- up_bias: float32 [4096], P('tensor'), may hold values from -2.5 to 2.5
- down_w: bfloat16 [4096, 1024], P('tensor'), may hold values from -0.09375 to 0.09375
- down_bias: float32 [1024], replicated, may hold values from -1.5 to 1.5
- cotangent: bfloat16 [32, 256, 1024], P('dp'), may hold values from -6 to 6
Outputs:
- output: bfloat16 [32, 256, 1024], P('dp')
- pixel_grad: float32 [32, 256, 768], P('dp')
- grad_embed: float32 [768, 1024], replicated
- grad_embed_bias: float32 [1024], replicated
- grad_norm_gain: float32 [2, 1024], replicated
- grad_norm_bias: float32 [2, 1024], replicated
- grad_qkv: float32 [3, 1024, 1024], P(None, None, 'tensor')
- grad_qv_bias: float32 [2, 1024], P(None, 'tensor')
- grad_out_proj: float32 [1024, 1024], P('tensor')
- grad_out_bias: float32 [1024], replicated
- grad_up: float32 [1024, 4096], P(None, 'tensor')
- grad_up_bias: float32 [4096], P('tensor')
- grad_down: float32 [4096, 1024], P('tensor')
- grad_down_bias: float32 [1024], replicated
Inputs may be any that keep to these rules, and one draw needn't show every extreme that they name: `patch_ids`: each row holds 256 distinct patch numbers of a 28 by 28 grid. `lengths`: the longest image has exactly 256 visible patches.
All inputs are finite; a program needn't handle non-finite values. No bound on the sum of `lengths` on one device may be relied on, other than what follows from the above.
Results may differ from a plain program's by a relative error of at most 0.013.
The roundings to bfloat16 on the way count: a program that leaves them out, or rounds other values in their place, can miss the bound.
Values sent between devices are 32-bit elements; how exact they have to be, the bound alone decides.
A program may use at most 192 MiB of HBM per device.

v0:
```python
import math

import jax
import jax.numpy as jnp
from jax import lax
from jax.sharding import PartitionSpec as P

HD = 64
GRID = 28


def positions(patch_ids, gsd_values, model_width, grid_side):
    quarter = model_width // 4
    gsd_scale = gsd_values.astype(jnp.float32) / 100.0
    row_pos = (patch_ids // grid_side).astype(jnp.float32) * gsd_scale[:, None]
    col_pos = (patch_ids % grid_side).astype(jnp.float32) * gsd_scale[:, None]
    frequency = jnp.exp(jnp.arange(quarter, dtype=jnp.float32) * (-math.log(10000.0) / quarter))
    row_angle = row_pos[:, :, None] * frequency
    col_angle = col_pos[:, :, None] * frequency
    return jnp.concatenate(
        [jnp.sin(row_angle), jnp.cos(row_angle), jnp.sin(col_angle), jnp.cos(col_angle)], axis=-1
    )


def contract_rows(left_side, right_side):
    return lax.dot_general(
        left_side, right_side, (((0,), (0,)), ((), ())), preferred_element_type=jnp.float32
    )


def contract_cols(left_side, right_side):
    return lax.dot_general(
        left_side, right_side, (((1,), (1,)), ((), ())), preferred_element_type=jnp.float32
    )


def normalize(hidden, gain_row, shift_row):
    centred = hidden - jnp.mean(hidden, axis=-1, keepdims=True)
    inverse = lax.rsqrt(jnp.mean(centred * centred, axis=-1, keepdims=True) + 1e-06)
    normed = centred * inverse
    return (normed * gain_row + shift_row, normed, inverse)


def normalize_back(upstream, normed, inverse, gain_row):
    scaled = upstream * gain_row
    return inverse * (
        scaled
        - jnp.mean(scaled, axis=-1, keepdims=True)
        - normed * jnp.mean(scaled * normed, axis=-1, keepdims=True)
    )


def gelu_slope(inputs):
    return 0.5 * (1.0 + lax.erf(inputs * (1.0 / math.sqrt(2.0)))) + inputs * jnp.exp(
        -0.5 * inputs * inputs
    ) * (1.0 / math.sqrt(2.0 * math.pi))


def per_device(
    pixels,
    lengths,
    patch_ids,
    gsd_values,
    embed_w,
    embed_bias,
    norm_gain,
    norm_bias,
    qkv_w,
    qv_bias,
    out_w,
    out_bias,
    up_w,
    up_bias,
    down_w,
    down_bias,
    cotangent,
):
    images, slot_count, patch_width = pixels.shape
    band_width = patch_width // 3
    model_width = embed_w.shape[1]
    local_width = qkv_w.shape[2]
    head_dim = HD
    heads_here = local_width // head_dim
    tokens = images * slot_count
    score_scale = 1.0 / math.sqrt(head_dim)
    key_keep = jnp.arange(slot_count)[None, :] < lengths[:, None]
    valid_rows = key_keep.astype(jnp.float32)
    pixel_grid = pixels.astype(jnp.float32).reshape(images, slot_count, 3, band_width)
    pixel_mask = valid_rows[:, :, None, None]
    total_one, total_two, band_count = lax.psum(
        (
            jnp.sum(pixel_grid * pixel_mask, axis=(0, 1, 3)),
            jnp.sum(pixel_grid * pixel_grid * pixel_mask, axis=(0, 1, 3)),
            jnp.sum(valid_rows) * band_width,
        ),
        "dp",
    )
    band_mean = total_one / band_count
    band_rstd = lax.rsqrt(total_two / band_count - band_mean * band_mean + 1e-05)
    pixel_hat = (pixel_grid - band_mean[:, None]) * band_rstd[:, None]
    pixel_low = pixel_hat.reshape(tokens, patch_width).astype(jnp.bfloat16)
    pos_table = positions(patch_ids, gsd_values, model_width, GRID).reshape(tokens, model_width)
    stream_zero = (
        jnp.dot(pixel_low, embed_w, preferred_element_type=jnp.float32) + embed_bias + pos_table
    )
    layer_one, normed_one, inverse_one = normalize(stream_zero, norm_gain[0], norm_bias[0])
    attn_input = layer_one.astype(jnp.bfloat16)
    queries = (
        jnp.dot(attn_input, qkv_w[0], preferred_element_type=jnp.float32) + qv_bias[0]
    ).astype(jnp.bfloat16)
    key_rows = jnp.dot(attn_input, qkv_w[1], preferred_element_type=jnp.float32).astype(
        jnp.bfloat16
    )
    values = (
        jnp.dot(attn_input, qkv_w[2], preferred_element_type=jnp.float32) + qv_bias[1]
    ).astype(jnp.bfloat16)
    query_heads = queries.reshape(images, slot_count, heads_here, head_dim)
    key_heads = key_rows.reshape(images, slot_count, heads_here, head_dim)
    value_heads = values.reshape(images, slot_count, heads_here, head_dim)

    def score_block():
        scores = (
            jnp.einsum(
                "ichd,ijhd->ihcj", query_heads, key_heads, preferred_element_type=jnp.float32
            )
            * score_scale
        )
        return jnp.where(key_keep[:, None, None, :], scores, -1e30)

    scores = score_block()
    top_score = jnp.max(scores, axis=-1, keepdims=True)
    exp_scores = jnp.exp(scores - top_score)
    exp_total = jnp.sum(exp_scores, axis=-1, keepdims=True)
    log_total = top_score + jnp.log(exp_total)
    prob_low = (exp_scores / exp_total).astype(jnp.bfloat16)
    attended = (
        jnp.einsum("ihcj,ijhd->ichd", prob_low, value_heads, preferred_element_type=jnp.float32)
        .astype(jnp.bfloat16)
        .reshape(tokens, local_width)
    )
    attn_out = lax.psum(jnp.dot(attended, out_w, preferred_element_type=jnp.float32), "tensor")
    stream_one = stream_zero + attn_out + out_bias
    layer_two, normed_two, inverse_two = normalize(stream_one, norm_gain[1], norm_bias[1])
    mlp_input = layer_two.astype(jnp.bfloat16)
    hidden_pre = jnp.dot(mlp_input, up_w, preferred_element_type=jnp.float32) + up_bias
    hidden_low = jax.nn.gelu(hidden_pre, approximate=False).astype(jnp.bfloat16)
    mlp_out = lax.psum(jnp.dot(hidden_low, down_w, preferred_element_type=jnp.float32), "tensor")
    stream_two = stream_one + mlp_out + down_bias
    row_valid = valid_rows.reshape(tokens, 1)
    output = (stream_two * row_valid).astype(jnp.bfloat16).reshape(images, slot_count, model_width)
    grad_two = cotangent.astype(jnp.float32).reshape(tokens, model_width) * row_valid
    grad_down_bias = jnp.sum(grad_two, axis=0)
    grad_two_low = grad_two.astype(jnp.bfloat16)
    grad_down = contract_rows(hidden_low, grad_two_low)
    grad_hidden = (contract_cols(grad_two_low, down_w) * gelu_slope(hidden_pre)).astype(
        jnp.bfloat16
    )
    grad_up = contract_rows(mlp_input, grad_hidden)
    grad_up_bias = jnp.sum(grad_hidden.astype(jnp.float32), axis=0)
    grad_mlp_in = lax.psum(contract_cols(grad_hidden, up_w), "tensor")
    grad_one = grad_two + normalize_back(grad_mlp_in, normed_two, inverse_two, norm_gain[1])
    grad_out_bias = jnp.sum(grad_one, axis=0)
    grad_one_low = grad_one.astype(jnp.bfloat16)
    grad_out_proj = contract_rows(attended, grad_one_low)
    grad_attended = (
        contract_cols(grad_one_low, out_w)
        .astype(jnp.bfloat16)
        .reshape(images, slot_count, heads_here, head_dim)
    )
    attn_probs = jnp.exp(score_block() - log_total)
    grad_probs = jnp.einsum(
        "ichd,ijhd->ihcj", grad_attended, value_heads, preferred_element_type=jnp.float32
    )
    grad_values = jnp.einsum(
        "ihcj,ichd->ijhd",
        attn_probs.astype(jnp.bfloat16),
        grad_attended,
        preferred_element_type=jnp.float32,
    ).astype(jnp.bfloat16)
    prob_dot = jnp.sum(attn_probs * grad_probs, axis=-1, keepdims=True)
    grad_scores = (attn_probs * (grad_probs - prob_dot)).astype(jnp.bfloat16)
    grad_queries = (
        jnp.einsum("ihcj,ijhd->ichd", grad_scores, key_heads, preferred_element_type=jnp.float32)
        * score_scale
    ).astype(jnp.bfloat16)
    grad_keys = (
        jnp.einsum("ihcj,ichd->ijhd", grad_scores, query_heads, preferred_element_type=jnp.float32)
        * score_scale
    ).astype(jnp.bfloat16)
    grad_proj = (
        grad_queries.reshape(tokens, local_width),
        grad_keys.reshape(tokens, local_width),
        grad_values.reshape(tokens, local_width),
    )
    grad_qkv = jnp.stack([contract_rows(attn_input, grad_piece) for grad_piece in grad_proj])
    grad_qv_bias = jnp.stack(
        [
            jnp.sum(grad_proj[0].astype(jnp.float32), axis=0),
            jnp.sum(grad_proj[2].astype(jnp.float32), axis=0),
        ]
    )
    attn_partial = (
        contract_cols(grad_proj[0], qkv_w[0])
        + contract_cols(grad_proj[1], qkv_w[1])
        + contract_cols(grad_proj[2], qkv_w[2])
    )
    grad_attn_in = lax.psum(attn_partial, "tensor")
    grad_zero = grad_one + normalize_back(grad_attn_in, normed_one, inverse_one, norm_gain[0])
    grad_norm_gain = jnp.stack(
        [jnp.sum(grad_attn_in * normed_one, axis=0), jnp.sum(grad_mlp_in * normed_two, axis=0)]
    )
    grad_norm_bias = jnp.stack([jnp.sum(grad_attn_in, axis=0), jnp.sum(grad_mlp_in, axis=0)])
    grad_embed_bias = jnp.sum(grad_zero, axis=0)
    grad_zero_low = grad_zero.astype(jnp.bfloat16)
    embed_part = contract_rows(pixel_low, grad_zero_low)
    grad_pixel_hat = contract_cols(grad_zero_low, embed_w).reshape(
        images, slot_count, 3, band_width
    )
    band_grad = jnp.sum(grad_pixel_hat, axis=(0, 1, 3))
    band_cross = jnp.sum(grad_pixel_hat * pixel_hat, axis=(0, 1, 3))
    (
        sum_qkv,
        sum_qv_bias,
        sum_out_proj,
        sum_out_bias,
        sum_up,
        sum_up_bias,
        sum_down,
        sum_down_bias,
        sum_gain,
        sum_shift,
        embed_sum,
        sum_embed_bias,
        band_grad_sum,
        band_cross_sum,
    ) = lax.psum(
        (
            grad_qkv,
            grad_qv_bias,
            grad_out_proj,
            grad_out_bias,
            grad_up,
            grad_up_bias,
            grad_down,
            grad_down_bias,
            grad_norm_gain,
            grad_norm_bias,
            embed_part,
            grad_embed_bias,
            band_grad,
            band_cross,
        ),
        "dp",
    )
    pixel_grad = band_rstd[:, None] * (
        grad_pixel_hat
        - pixel_mask * (band_grad_sum[:, None] + band_cross_sum[:, None] * pixel_hat) / band_count
    )
    pixel_grad = pixel_grad.reshape(images, slot_count, patch_width)
    return (
        output,
        pixel_grad,
        embed_sum,
        sum_embed_bias,
        sum_gain,
        sum_shift,
        sum_qkv,
        sum_qv_bias,
        sum_out_proj,
        sum_out_bias,
        sum_up,
        sum_up_bias,
        sum_down,
        sum_down_bias,
    )


def solution(mesh):
    in_specs = (
        P("dp", None, None),
        P("dp"),
        P("dp", None),
        P("dp"),
        P(),
        P(),
        P(),
        P(),
        P(None, None, "tensor"),
        P(None, "tensor"),
        P("tensor", None),
        P(),
        P(None, "tensor"),
        P("tensor"),
        P("tensor", None),
        P(),
        P("dp", None, None),
    )
    out_specs = (
        P("dp", None, None),
        P("dp", None, None),
        P(),
        P(),
        P(),
        P(),
        P(None, None, "tensor"),
        P(None, "tensor"),
        P("tensor", None),
        P(),
        P(None, "tensor"),
        P("tensor"),
        P("tensor", None),
        P(),
    )
    return jax.shard_map(
        per_device, mesh=mesh, in_specs=in_specs, out_specs=out_specs, check_vma=False
    )
```

profile of v0, /device:TPU:0, one launch (start us, length us, event | category | flops | bytes accessed | tf_op | source)
XLA Modules:
  0.0 888.7 jit_solution(13211194618216257709)
XLA Ops:
  7.3 1.4 convert_reduce_fusion.3
  11.6 1.5 multiply_reduce_fusion.11
  14.0 35.5 %all-reduce.1 = (f32[3]{0:T(128)S(1)}, f32[]{:T(128)}, f32[3]{0:T(128)S(1)}) all-reduce(f32[3]{0:T(128)S(1)} %reduce_sum.255, f32[]{:T(128)S(6)} %mul.305, f32[3]{0:T(128)S(1)} %reduce_sum.259), channel_id=1, replica_groups=mesh['dp'=16,'tensor'=2] {'dp'}, use_global_device_ids=true, to_apply=%region_2.0 | all-reduce | flops 7 | bytes 56 | tf_op jit(solution)/shard_map/psum | solution.py:90
  50.3 0.8 fusion.70
  51.1 0.8 fusion.71
  51.9 1.3 fusion.24
  53.2 3.7 multiply_sine_fusion.1
  57.0 1.1 fusion.73
  59.4 1.3 copy-done.29
  60.7 1.5 convolution_convert_fusion.1
  62.9 1.5 fusion.25
  64.4 2.4 reshape.237
  66.8 2.5 copy.68
  69.3 1.5 reshape.238
  70.8 1.7 copy.66
  72.5 2.8 reshape.239
  75.3 2.5 copy.67
  77.8 2.1 fusion.74
  80.5 1.4 copy-done.1
  81.9 0.9 fusion.35
  83.5 0.8 copy-done.15
  84.3 2.0 fusion.75
  86.4 2.4 fusion.22
  88.8 57.9 %all-reduce.9.cloned.1.call-done = f32[512,1024]{1,0:T(8,128)} async-done(((f32[512,1024]{1,0:T(8,128)}), f32[512,1024]{1,0:T(8,128)}) %all-reduce.9.cloned.1.call-update) | async-done | bytes 2097168 | tf_op jit(solution)/shard_map/psum | solution.py:141
  146.7 2.7 fusion.69
  150.3 12.6 %fusion.2 = (bf16[512,2048]{1,0:T(8,128)(2,1)}, f32[512,2048]{1,0:T(8,128)S(1)}) fusion(f32[2048]{0:T(1024)S(1)} %copy-done.40, bf16[1024,2048]{1,0:T(8,128)(2,1)S(1)} %copy-done.38, f32[512,1024]{1,0:T(8,128)S(1)} %get-tuple-element.50, f32[1024]{0:T(1024)S(1)} %bitcast.162, f32[1024]{0:T(1024)S(1)} %bitcast.148, f32[512]{0:T(512)S(1)} %add_rsqrt_fusion, ...), kind=kOutput, calls=%fused_computation.5 | convolution fusion | flops 2219311104 | bytes 12603392 | tf_op jit(solution)/shard_map/dot_general | solution.py:145
  162.9 3.8 convert_reduce_fusion
  166.8 1.3 copy-done.42
  168.1 3.7 fusion.77
  171.8 8.8 all-reduce.15.cloned.1.call-start
  180.6 6.5 fusion.76
  187.1 47.8 %all-reduce.11.cloned.1.call-done = f32[512,1024]{1,0:T(8,128)} async-done(((f32[512,1024]{1,0:T(8,128)}), f32[512,1024]{1,0:T(8,128)}) %all-reduce.11.cloned.1.call-update) | async-done | bytes 2097168 | tf_op jit(solution)/shard_map/psum | solution.py:160
  234.9 3.2 multiply_reduce_fusion.2
  238.2 2.5 fusion.67
  240.7 1.3 copy-done.8
  242.8 1.5 reshape.240
  244.3 1.7 copy.72
  246.0 3.2 convert_reduce_fusion.1
  249.6 1.0 multiply_reduce_fusion
  250.6 1.0 multiply_convert_fusion
  255.2 0.8 copy-done.30
  257.6 2.4 add_add_fusion
  260.0 7.9 fusion.78
  267.9 6.0 fusion.64
  276.6 3.4 pad_maximum_fusion
  280.0 2.0 fusion.57
  282.0 86.0 %all-reduce.15.cloned.1.call-done = (f32[512,1024]{1,0:T(8,128)}, f32[512,1024]{1,0:T(8,128)}) async-done(((f32[512,1024]{1,0:T(8,128)}, f32[512,1024]{1,0:T(8,128)}), (f32[512,1024]{1,0:T(8,128)}, f32[512,1024]{1,0:T(8,128)})) %all-reduce.15.cloned.1.call-update) | async-done | bytes 4194320 | tf_op jit(solution)/shard_map/psum | solution.py:147
  368.0 3.2 multiply_reduce_fusion.3
  371.5 2.4 fusion.68
  373.9 1.0 copy-done.28
  374.9 2.7 fusion.53
  377.6 1.2 copy-done.12
  379.2 3.4 fusion.66
  382.9 65.1 %all-reduce = (f32[3]{0:T(128)S(1)}, f32[3]{0:T(128)S(1)}, f32[1024]{0:T(1024)}, f32[2,1024]{1,0:T(2,128)}, f32[2,1024]{1,0:T(2,128)}, /*index=5*/f32[2,512]{1,0...) all-reduce(f32[3]{0:T(128)S(1)} %reduce_sum.275, ...), channel_id=1, replica_groups=mesh['dp'=16,'tensor'=2] {'dp'}, use_global_device_ids=true, to_apply=%region_28.29 | all-reduce | flops 10246 | bytes 81968 | tf_op jit(solution)/shard_map/psum | solution.py:236
  448.2 3.7 multiply_convert_fusion.1
  452.0 2.3 subtract_multiply_fusion.2
  454.2 407.6 %all-reduce.13.cloned.1.call-done = (f32[768,1024]{1,0:T(8,128)}, f32[3,1024,512]{2,1,0:T(8,128)}, f32[512,1024]{1,0:T(8,128)}, f32[1024,2048]{1,0:T(8,128)}, f32[2048,1024]{1,0:T(8,128)}) async-done(((f32[768,1024]{1,0:T(8,128)}, f32[3,1024,512]{2,1,0:T(8,128)}, f32[512,1024]{1,0:T(8,128)}, f32[1024,2048]{1,0:T(8,128)}, f32[2048,1024]{1,0:T(8,128)}), (f32[768,1024]{1,0:T(8,128)}, ...) | async-done | bytes 28311568 | tf_op jit(solution)/shard_map/psum | solution.py:236
  861.9 4.1 copy.111
  866.3 3.2 copy.112
  869.5 1.3 copy-done.33
  870.8 1.3 copy.113
  872.7 4.3 copy.114
  877.0 1.4 slice-done.1
  878.4 3.4 copy.115
  (155 shorter events, 19.1 us)
Async XLA Ops:
  7.2 49.8 %copy-start = (bf16[768,1024]{1,0:T(8,128)(2,1)S(1)}, bf16[768,1024]{1,0:T(8,128)(2,1)}, u32[]{:S(2)}) copy-start(bf16[768,1024]{1,0:T(8,128)(2,1)} %param.21) | copy-start | bytes 4718596
  7.2 139.5 %all-reduce.9.cloned.1.call-start = ((), (), s32[]{:S(2)}) async-start(), calls=%async_computation | async-start | bytes 4194304 | tf_op jit(solution)/shard_map/psum | solution.py:141
  13.1 43.8 %copy-start.41 = (f32[1024]{0:T(1024)S(1)}, f32[1024]{0:T(1024)}, u32[]{:S(2)}) copy-start(f32[1024]{0:T(1024)} %param.22) | copy-start | bytes 12292
  53.2 4.9 copy-start.24
  58.1 1.3 copy-start.3
  58.4 2.3 copy-start.29
  72.5 7.4 copy-start.19
  79.9 2.0 copy-start.1
  79.9 2.0 copy-start.31
  82.8 1.5 copy-start.26
  83.5 0.8 copy-start.15
  86.3 60.4 %copy-start.36 = (f32[1024]{0:T(1024)S(1)}, f32[1024]{0:T(1024)}, u32[]{:S(2)}) copy-start(f32[1024]{0:T(1024)} %param.28) | copy-start | bytes 12292
  86.3 148.6 %all-reduce.11.cloned.1.call-start = ((), (), s32[]{:S(2)}) async-start(), calls=%async_computation.1 | async-start | bytes 4194304 | tf_op jit(solution)/shard_map/psum | solution.py:160
  146.7 3.4 copy-start.38
  149.4 13.5 %copy-start.5 = (f32[512,1024]{1,0:T(8,128)}, f32[512,1024]{1,0:T(8,128)S(1)}, u32[]{:S(2)}) copy-start(f32[512,1024]{1,0:T(8,128)S(1)} %get-tuple-element.50) | copy-start | bytes 6291460
  149.4 0.9 copy-start.40
  150.3 12.6 %copy-start.35 = (bf16[512,1024]{1,0:T(8,128)(2,1)S(1)}, bf16[512,1024]{1,0:T(8,128)(2,1)}, u32[]{:S(2)}) copy-start(bf16[512,1024]{1,0:T(8,128)(2,1)} %fusion.22) | copy-start | bytes 3145732
  150.3 12.6 %copy-start.39 = (bf16[2048,1024]{1,0:T(8,128)(2,1)S(1)}, bf16[2048,1024]{1,0:T(8,128)(2,1)}, u32[]{:S(2)}) copy-start(bf16[2048,1024]{1,0:T(8,128)(2,1)} %param.31) | copy-start | bytes 12582916
  166.8 1.3 copy-start.42
  171.8 196.2 %all-reduce.15.cloned.1.call-start = ((), (), s32[]{:S(2)}) async-start(), calls=%async_computation.3 | async-start | bytes 8388608 | tf_op jit(solution)/shard_map/psum | solution.py:147
  234.9 3.3 copy-start.6
  234.9 3.3 copy-start.11
  238.2 3.8 copy-start.27
  240.7 1.3 copy-start.8
  246.0 3.5 copy-start.2
  246.0 3.6 copy-start.32
  250.6 1.0 copy-start.20
  251.7 1.0 copy-start.21
  253.9 3.6 copy-start.22
  253.9 2.1 copy-start.30
  255.2 2.3 copy-start.17
  260.0 601.9 %all-reduce.13.cloned.1.call-start = ((), (), s32[]{:S(2)}) async-start(), calls=%async_computation.2 | async-start | bytes 56623104 | tf_op jit(solution)/shard_map/psum | solution.py:236
  260.0 7.9 copy-start.7
  260.0 7.9 copy-start.43
  267.9 6.0 copy-start.23
  273.9 1.1 copy-start.18
  276.5 3.5 copy-start.9
  276.6 3.5 copy-start.16
  368.0 3.3 copy-start.4
  368.0 3.5 copy-start.10
  371.5 3.4 copy-start.25
  373.9 1.0 copy-start.28
  377.6 1.2 copy-start.12
  377.6 1.7 copy-start.13
  379.2 69.0 %copy-start.37 = (f32[1024]{0:T(1024)S(1)}, f32[1024]{0:T(1024)}, u32[]{:S(2)}) copy-start(f32[1024]{0:T(1024)} %param.32) | copy-start | bytes 12292
  448.2 3.7 copy-start.34
  861.9 4.4 copy-start.14
  861.9 10.3 %slice-start.2 = ((s8[8388608]{0:T(1024)(128)(4,1)}), s8[4194304]{0:T(1024)(128)(4,1)S(1)}, s32[]{:S(2)}) async-start(s8[8388608]{0:T(1024)(128)(4,1)} %bitcast.129), calls=%async_computation.6 | async-start | bytes 8388608
  866.3 4.5 copy-start.33
  866.3 6.4 slice-start.3
  870.8 6.1 slice-start
  872.7 5.7 slice-start.1
Sparse Core Ops, SparseCore 0:
  86.4 60.2 all-reduce.8
  171.9 62.9 all-reduce.10
  260.1 107.9 all-reduce.14
  377.7 484.1 all-reduce.12
where the time goes:
time: 897 us; the launch traced here: 889 us
  waiting for transfers between devices  599 us (67%)
  blocking collectives  101 us (11%)
  matrix products  70.8 us (8%)
  local copies, waits for them, and re-layouts  53.3 us (6%)
  other arithmetic  40.2 us (4%)
  between operations  15.5 us (2%)
    psum x1, waiting for transfers between devices, per_device(): lax.psum((grad_qkv, grad_qv_bias, grad_out_proj, grad_out_bias, grad_up,...  408 us
    psum x1, waiting for transfers between devices, per_device(): lax.psum(jnp.dot(hidden_low, down_w, preferred_element_type=jnp.float32),...  86 us
    psum x1, blocking collectives, per_device(): lax.psum((grad_qkv, grad_qv_bias, grad_out_proj, grad_out_bias, grad_up,...  65.1 us
    psum x1, waiting for transfers between devices, per_device(): lax.psum(jnp.dot(attended, out_w, preferred_element_type=jnp.float32), 't...  57.9 us
    psum x1, waiting for transfers between devices, per_device(): grad_mlp_in = lax.psum(contract_cols(grad_hidden, up_w), 'tensor')  47.8 us
    psum x1, blocking collectives, per_device(): lax.psum((jnp.sum(pixel_grid * pixel_mask, axis=(0, 1, 3)), jnp.sum(pixel...  35.5 us
    unnamed x108, local copies, waits for them, and re-layouts  31.7 us
    dot_general x7, matrix products, contract_rows(): lax.dot_general(left_side, right_side, (((0,), (0,)), ((), ())), preferre...  20.9 us
  transfers between devices with their start and end apart: 4, of which 4 were waited for; matrix products, arithmetic and copies ran while one was open for 5% of the time, Pallas kernels for 0%

commit v1 on v0

--- a/solution.py
+++ b/solution.py
@@ -1,12 +1,289 @@
+import functools
 import math
 
 import jax
 import jax.numpy as jnp
 from jax import lax
+from jax.experimental import pallas as pl
+from jax.experimental.pallas import tpu as pltpu
 from jax.sharding import PartitionSpec as P
 
 HD = 64
 GRID = 28
+MESH = pl.DeviceIdType.MESH
+W = 512
+
+
+SEND = ("c","x","oa","ob","ja","jb","xb","ga","gb","na","fa","nb","fb","xg","cg")
+
+def dp_kernel(shapes, R, K, delays, *refs):
+    n = len(shapes)
+    ins, outs = refs[:n], refs[n:2*n]
+    own, cl, xl, ab, oa, ob, ja, jb, nbuf, xbl, fin, ssem, rsem, lsem = refs[2*n:]
+    H, Q, E = R//2, R//4, R//8
+    i = lax.axis_index("dp"); t = lax.axis_index("tensor")
+    c = lax.rem(i, 2); x = lax.rem(i//2, 2); z = i//4
+    side = z//2
+    pos = lax.rem(z, 2)
+    inner = lax.rem(side + pos, 2) == 1
+    outer = lax.rem(side + pos, 2) == 0
+    dev_c = (z*4 + x*2 + 1 - c, t)
+    dev_x = (z*4 + (1-x)*2 + c, t)
+    dev_o = ((side*2 + 1 - pos)*4 + x*2 + c, t)
+    dev_j = ((3 - z)*4 + x*2 + c, t)
+    bar = pltpu.get_barrier_semaphore()
+    for d in (dev_c, dev_x, dev_o):
+        pl.semaphore_signal(bar, inc=1, device_id=d, device_id_type=MESH)
+    @pl.when(inner)
+    def _():
+        pl.semaphore_signal(bar, inc=1, device_id=dev_j, device_id_type=MESH)
+        pl.semaphore_wait(bar, 4)
+    @pl.when(outer)
+    def _():
+        pl.semaphore_wait(bar, 3)
+    starts, total = [], 0
+    for (rows, cols) in shapes:
+        starts.append(total); total += (rows//(2*R))*(cols//W)
+    NC = total
+    def al(v, m): return pl.multiple_of(v, m)
+    def slot(j): return lax.rem(j, K)
+    a_mine = al(x*Q, Q); a_other = al((1-x)*Q, Q)
+    e_near = al(side*E, E); e_far = al((1-side)*E, E)
+    b_near = al(H + side*Q, Q); b_far = al(H + (1-side)*Q, Q)
+    aN = al(x*Q + side*E, E); aF = al(x*Q + (1-side)*E, E)
+    def hbm(ref, a, j, half):
+        cols = shapes[a][1]//W
+        q = j - starts[a]
+        r = al((q//cols)*(2*R) + half*R, R)
+        col = al(lax.rem(q, cols)*W, W)
+        return ref.at[pl.ds(r, R), pl.ds(col, W)]
+    def rc(kind, src, dst, dev, s):
+        k = SEND.index(kind)
+        return pltpu.make_async_remote_copy(src_ref=src, dst_ref=dst, send_sem=ssem.at[k, s], recv_sem=rsem.at[k, s], device_id=dev, device_id_type=MESH)
+    def desc(kind, j):
+        s = slot(j)
+        if kind == "x": return rc(kind, own.at[s, pl.ds(a_other, Q)], xl.at[s], dev_x, s)
+        if kind == "ob": return rc(kind, own.at[s, pl.ds(H, H)], ob.at[s], dev_o, s)
+        if kind == "oa": return rc(kind, ab.at[s], oa.at[s], dev_o, s)
+        if kind == "ja": return rc(kind, ab.at[s, pl.ds(e_far, E)], ja.at[s], dev_j, s)
+        if kind == "jb": return rc(kind, own.at[s, pl.ds(b_far, Q)], jb.at[s], dev_j, s)
+        if kind == "xb": return rc(kind, nbuf.at[s], xbl.at[s], dev_x, s)
+        if kind in ("ga", "na"):
+            return rc(kind, fin.at[s, pl.ds(aN, E)], fin.at[s, pl.ds(aN, E)], dev_j if kind == "ga" else dev_o, s)
+        if kind == "fa": return rc(kind, fin.at[s, pl.ds(aF, E)], fin.at[s, pl.ds(aF, E)], dev_o, s)
+        if kind in ("gb", "nb"):
+            return rc(kind, fin.at[s, pl.ds(b_near, Q)], fin.at[s, pl.ds(b_near, Q)], dev_j if kind == "gb" else dev_o, s)
+        if kind == "fb": return rc(kind, fin.at[s, pl.ds(b_far, Q)], fin.at[s, pl.ds(b_far, Q)], dev_o, s)
+        if kind == "xg": return rc(kind, fin.at[s, pl.ds(a_mine, Q)], fin.at[s, pl.ds(a_mine, Q)], dev_x, s)
+        if kind == "c": return rc(kind, hbm(ins[0], 0, starts[0], 1 - c), cl.at[s], dev_c, s)
+        if kind == "cg": return rc(kind, fin.at[s], hbm(outs[0], 0, starts[0], c), dev_c, s)
+        raise ValueError(kind)
+    def each(j, f):
+        for a in range(n):
+            end = starts[a+1] if a + 1 < n else NC
+            if n == 1: f(a); continue
+            cond = (j >= starts[a]) & (j < end)
+            pl.when(cond)(functools.partial(f, a))
+    d = delays
+    def step(tt, carry):
+        js = [tt - dd for dd in d]
+        def on(k): return (js[k] >= 0) & (js[k] < NC)
+        @pl.when(on(7))
+        def _():
+            j = js[7]; s = slot(j)
+            pltpu.make_async_copy(fin.at[s], hbm(outs[0], 0, starts[0], c), lsem.at[1, s]).wait()
+            desc("cg", j).wait_send(); desc("cg", j).wait_recv()
+            desc("c", j).wait_send(); desc("x", j).wait_send(); desc("xg", j).wait_send()
+            @pl.when(outer)
+            def _():
+                desc("oa", j).wait_send(); desc("ob", j).wait_send()
+            @pl.when(inner)
+            def _():
+                for k in ("ja","jb","xb","ga","gb","na","fa","nb","fb"): desc(k, j).wait_send()
+        @pl.when(on(6))
+        def _():
+            j = js[6]
+            desc("xg", j).wait_recv()
+            @pl.when(outer)
+            def _():
+                desc("nb", j).wait_recv(); desc("fb", j).wait_recv()
+        @pl.when(on(5))
+        def _():
+            j = js[5]
+            @pl.when(inner)
+            def _():
+                desc("ga", j).wait_recv(); desc("gb", j).wait_recv()
+        j5o = tt - d[5] - d[8]
+        on5o = (j5o >= 0) & (j5o < NC)
+        @pl.when(on5o & outer)
+        def _():
+            desc("na", j5o).wait_recv(); desc("fa", j5o).wait_recv()
+        @pl.when(on(4))
+        def _():
+            j = js[4]; s = slot(j)
+            @pl.when(inner)
+            def _():
+                desc("ja", j).wait_recv(); desc("xb", j).wait_recv()
+                fin[s, pl.ds(aN, E)] = ab[s, pl.ds(e_near, E)] + ja[s]
+                fin[s, pl.ds(b_near, Q)] = nbuf[s] + xbl[s]
+        @pl.when(on(3))
+        def _():
+            j = js[3]; s = slot(j)
+            @pl.when(inner)
+            def _():
+                desc("oa", j).wait_recv(); desc("jb", j).wait_recv()
+                ab[s] = ab[s] + oa[s]
+                nbuf[s] = own[s, pl.ds(b_near, Q)] + jb[s]
+        @pl.when(on(2))
+        def _():
+            j = js[2]; s = slot(j)
+            desc("x", j).wait_recv()
+            ab[s] = own[s, pl.ds(a_mine, Q)] + xl[s]
+            @pl.when(inner)
+            def _():
+                desc("ob", j).wait_recv()
+                own[s, pl.ds(H, H)] = own[s, pl.ds(H, H)] + ob[s]
+        @pl.when(on(1))
+        def _():
+            j = js[1]; s = slot(j)
+            pltpu.make_async_copy(hbm(ins[0], 0, starts[0], c), own.at[s], lsem.at[0, s]).wait()
+            desc("c", j).wait_recv()
+            own[s] = own[s] + cl[s]
+        @pl.when(on(6))
+        def _():
+            j = js[6]; s = slot(j)
+            def f(a):
+                pltpu.make_async_copy(fin.at[s], hbm(outs[a], a, j, c), lsem.at[1, s]).start()
+                rc("cg", fin.at[s], hbm(outs[a], a, j, c), dev_c, s).start()
+            each(j, f)
+        @pl.when(on(5))
+        def _():
+            j = js[5]
+            @pl.when(inner)
+            def _():
+                desc("fa", j).start(); desc("xg", j).start(); desc("fb", j).start()
+        @pl.when(on5o & outer)
+        def _():
+            desc("xg", j5o).start()
+        @pl.when(on(4))
+        def _():
+            j = js[4]
+            @pl.when(inner)
+            def _():
+                for k in ("ga","na","gb","nb"): desc(k, j).start()
+        @pl.when(on(3))
+        def _():
+            j = js[3]
+            @pl.when(inner)
+            def _():
+                desc("ja", j).start(); desc("xb", j).start()
+        @pl.when(on(2))
+        def _():
+            j = js[2]
+            @pl.when(outer)
+            def _(): desc("oa", j).start()
+            @pl.when(inner)
+            def _(): desc("jb", j).start()
+        @pl.when(on(1))
+        def _():
+            j = js[1]
+            desc("x", j).start()
+            @pl.when(outer)
+            def _(): desc("ob", j).start()
+        @pl.when(on(0))
+        def _():
+            j = js[0]; s = slot(j)
+            def f(a):
+                pltpu.make_async_copy(hbm(ins[a], a, j, c), own.at[s], lsem.at[0, s]).start()
+                rc("c", hbm(ins[a], a, j, 1 - c), cl.at[s], dev_c, s).start()
+            each(j, f)
+        return carry
+    lax.fori_loop(0, NC + d[7], step, 0)
+
+def dp_sum(arrays, R=64, K=16, delays=(0,1,3,5,7,9,12,13,1), name="dp_sum", cid=1):
+    shapes = tuple(a.shape for a in arrays)
+    n = len(arrays)
+    H, Q, E = R//2, R//4, R//8
+    f32 = jnp.float32
+    V = lambda r: pltpu.VMEM((K, r, W), f32)
+    return pl.pallas_call(
+        functools.partial(dp_kernel, shapes, R, K, delays),
+        out_shape=[jax.ShapeDtypeStruct(s, f32) for s in shapes],
+        in_specs=[pl.BlockSpec(memory_space=pl.ANY)]*n,
+        out_specs=[pl.BlockSpec(memory_space=pl.ANY)]*n,
+        scratch_shapes=[V(R), V(R), V(Q), V(Q), V(Q), V(H), V(E), V(Q), V(Q), V(Q), V(R),
+            pltpu.SemaphoreType.DMA((len(SEND), K)), pltpu.SemaphoreType.DMA((len(SEND), K)), pltpu.SemaphoreType.DMA((2, K))],
+        compiler_params=pltpu.CompilerParams(collective_id=cid, has_side_effects=True, vmem_limit_bytes=40 << 20),
+        name=name)(*arrays)
+
+
+def stats_kernel(ranks, band_width, lens, pix, out, mine, table, ssem, rsem):
+    me = lax.axis_index("dp")
+    t = lax.axis_index("tensor")
+    bar = pltpu.get_barrier_semaphore()
+    for k in range(1, ranks):
+        pl.semaphore_signal(bar, inc=1, device_id=(lax.rem(me + k, ranks), t), device_id_type=MESH)
+    images, slots, width = pix.shape
+    one = jnp.zeros((1, width), jnp.float32)
+    two = jnp.zeros((1, width), jnp.float32)
+    number = jnp.zeros((1, width), jnp.float32)
+    for k in range(images):
+        keep = (lax.broadcasted_iota(jnp.int32, (slots, 1), 0) < lens[k]).astype(jnp.float32)
+        x = pix[k].astype(jnp.float32)
+        kept = x * keep
+        one = one + jnp.sum(kept, axis=0, keepdims=True)
+        two = two + jnp.sum(kept * x, axis=0, keepdims=True)
+        number = number + jnp.sum(keep, axis=0, keepdims=True)
+    mine[...] = jnp.concatenate([one, two, number, jnp.zeros((5, width), jnp.float32)], axis=0)
+    pl.semaphore_wait(bar, ranks - 1)
+
+    def copy(k):
+        peer = lax.rem(me + k, ranks)
+        return pltpu.make_async_remote_copy(
+            src_ref=mine, dst_ref=table.at[me], send_sem=ssem.at[k - 1], recv_sem=rsem.at[me],
+            device_id=(peer, t), device_id_type=MESH)
+
+    def arrival(k):
+        peer = lax.rem(me + k, ranks)
+        return pltpu.make_async_remote_copy(
+            src_ref=mine, dst_ref=table.at[peer], send_sem=ssem.at[k - 1], recv_sem=rsem.at[peer],
+            device_id=(peer, t), device_id_type=MESH)
+
+    for k in range(1, ranks):
+        copy(k).start()
+    table[me] = mine[...]
+    for k in range(1, ranks):
+        arrival(k).wait_recv()
+    total = table[0]
+    for k in range(1, ranks):
+        total = total + table[k]
+    for k in range(1, ranks):
+        copy(k).wait_send()
+    for b in range(width // band_width):
+        cols = slice(b * band_width, (b + 1) * band_width)
+        count = total[2:3, cols] * float(band_width)
+        mean = jnp.sum(total[0:1, cols], axis=1, keepdims=True) / count
+        square = jnp.sum(total[1:2, cols], axis=1, keepdims=True) / count
+        rstd = lax.rsqrt(square - mean * mean + 1e-05)
+        out[:, cols] = jnp.concatenate(
+            [mean, rstd, count, jnp.zeros((5, band_width), jnp.float32)], axis=0)
+
+
+def band_stats(pixels, lengths, ranks):
+    width = pixels.shape[2]
+    return pl.pallas_call(
+        functools.partial(stats_kernel, ranks, width // 3),
+        out_shape=jax.ShapeDtypeStruct((8, width), jnp.float32),
+        in_specs=[pl.BlockSpec(memory_space=pltpu.SMEM), pl.BlockSpec(memory_space=pltpu.VMEM)],
+        out_specs=pl.BlockSpec(memory_space=pltpu.VMEM),
+        scratch_shapes=[
+            pltpu.VMEM((8, width), jnp.float32),
+            pltpu.VMEM((ranks, 8, width), jnp.float32),
+            pltpu.SemaphoreType.DMA((ranks,)),
+            pltpu.SemaphoreType.DMA((ranks,)),
+        ],
+        compiler_params=pltpu.CompilerParams(collective_id=2, has_side_effects=True),
+        name="band_stats")(lengths, pixels)
 
 
 def positions(patch_ids, gsd_values, model_width, grid_side):
@@ -56,7 +333,14 @@
     ) * (1.0 / math.sqrt(2.0 * math.pi))
 
 
+def tensor_sum(part):
+    if lax.axis_size("tensor") != 2:
+        return lax.psum(part, "tensor")
+    return part + lax.ppermute(part, "tensor", [(0, 1), (1, 0)])
+
+
 def per_device(
+    fast,
     pixels,
     lengths,
     patch_ids,
@@ -87,16 +371,22 @@
     valid_rows = key_keep.astype(jnp.float32)
     pixel_grid = pixels.astype(jnp.float32).reshape(images, slot_count, 3, band_width)
     pixel_mask = valid_rows[:, :, None, None]
-    total_one, total_two, band_count = lax.psum(
-        (
-            jnp.sum(pixel_grid * pixel_mask, axis=(0, 1, 3)),
-            jnp.sum(pixel_grid * pixel_grid * pixel_mask, axis=(0, 1, 3)),
-            jnp.sum(valid_rows) * band_width,
-        ),
-        "dp",
-    )
-    band_mean = total_one / band_count
-    band_rstd = lax.rsqrt(total_two / band_count - band_mean * band_mean + 1e-05)
+    if fast:
+        stats = band_stats(pixels, lengths, 16)
+        band_mean = stats[0].reshape(3, band_width)[:, 0]
+        band_rstd = stats[1].reshape(3, band_width)[:, 0]
+        band_count = stats[2, 0]
+    else:
+        total_one, total_two, band_count = lax.psum(
+            (
+                jnp.sum(pixel_grid * pixel_mask, axis=(0, 1, 3)),
+                jnp.sum(pixel_grid * pixel_grid * pixel_mask, axis=(0, 1, 3)),
+                jnp.sum(valid_rows) * band_width,
+            ),
+            "dp",
+        )
+        band_mean = total_one / band_count
+        band_rstd = lax.rsqrt(total_two / band_count - band_mean * band_mean + 1e-05)
     pixel_hat = (pixel_grid - band_mean[:, None]) * band_rstd[:, None]
     pixel_low = pixel_hat.reshape(tokens, patch_width).astype(jnp.bfloat16)
     pos_table = positions(patch_ids, gsd_values, model_width, GRID).reshape(tokens, model_width)
@@ -138,16 +428,14 @@
         .astype(jnp.bfloat16)
         .reshape(tokens, local_width)
     )
-    attn_out = lax.psum(jnp.dot(attended, out_w, preferred_element_type=jnp.float32), "tensor")
+    attn_out = tensor_sum(jnp.dot(attended, out_w, preferred_element_type=jnp.float32))
     stream_one = stream_zero + attn_out + out_bias
     layer_two, normed_two, inverse_two = normalize(stream_one, norm_gain[1], norm_bias[1])
     mlp_input = layer_two.astype(jnp.bfloat16)
     hidden_pre = jnp.dot(mlp_input, up_w, preferred_element_type=jnp.float32) + up_bias
     hidden_low = jax.nn.gelu(hidden_pre, approximate=False).astype(jnp.bfloat16)
-    mlp_out = lax.psum(jnp.dot(hidden_low, down_w, preferred_element_type=jnp.float32), "tensor")
-    stream_two = stream_one + mlp_out + down_bias
+    mlp_part = jnp.dot(hidden_low, down_w, preferred_element_type=jnp.float32)
     row_valid = valid_rows.reshape(tokens, 1)
-    output = (stream_two * row_valid).astype(jnp.bfloat16).reshape(images, slot_count, model_width)
     grad_two = cotangent.astype(jnp.float32).reshape(tokens, model_width) * row_valid
     grad_down_bias = jnp.sum(grad_two, axis=0)
     grad_two_low = grad_two.astype(jnp.bfloat16)
@@ -157,7 +445,7 @@
     )
     grad_up = contract_rows(mlp_input, grad_hidden)
     grad_up_bias = jnp.sum(grad_hidden.astype(jnp.float32), axis=0)
-    grad_mlp_in = lax.psum(contract_cols(grad_hidden, up_w), "tensor")
+    grad_mlp_in = tensor_sum(contract_cols(grad_hidden, up_w))
     grad_one = grad_two + normalize_back(grad_mlp_in, normed_two, inverse_two, norm_gain[1])
     grad_out_bias = jnp.sum(grad_one, axis=0)
     grad_one_low = grad_one.astype(jnp.bfloat16)
@@ -204,7 +492,10 @@
         + contract_cols(grad_proj[1], qkv_w[1])
         + contract_cols(grad_proj[2], qkv_w[2])
     )
-    grad_attn_in = lax.psum(attn_partial, "tensor")
+    grad_attn_in = tensor_sum(attn_partial)
+    mlp_part, _ = lax.optimization_barrier((mlp_part, grad_attn_in))
+    stream_two = stream_one + tensor_sum(mlp_part) + down_bias
+    output = (stream_two * row_valid).astype(jnp.bfloat16).reshape(images, slot_count, model_width)
     grad_zero = grad_one + normalize_back(grad_attn_in, normed_one, inverse_one, norm_gain[0])
     grad_norm_gain = jnp.stack(
         [jnp.sum(grad_attn_in * normed_one, axis=0), jnp.sum(grad_mlp_in * normed_two, axis=0)]
@@ -218,40 +509,42 @@
     )
     band_grad = jnp.sum(grad_pixel_hat, axis=(0, 1, 3))
     band_cross = jnp.sum(grad_pixel_hat * pixel_hat, axis=(0, 1, 3))
+    small = (
+        grad_qv_bias,
+        grad_out_bias,
+        grad_up_bias,
+        grad_down_bias,
+        grad_norm_gain,
+        grad_norm_bias,
+        grad_embed_bias,
+        band_grad,
+        band_cross,
+    )
+    large = (grad_qkv.reshape(-1, local_width), grad_out_proj, grad_up, grad_down, embed_part)
+    if fast:
+        packed = jnp.concatenate([piece.reshape(-1) for piece in small])
+        packed = jnp.pad(packed, (0, 128 * W - packed.shape[0])).reshape(128, W)
+        *large, packed = dp_sum((*large, packed))
+        flat, at, pieces = packed.reshape(-1), 0, []
+        for piece in small:
+            pieces.append(flat[at : at + piece.size].reshape(piece.shape))
+            at += piece.size
+        small = pieces
+    else:
+        large, small = lax.psum((large, small), "dp")
+    sum_qkv, sum_out_proj, sum_up, sum_down, embed_sum = large
+    sum_qkv = sum_qkv.reshape(grad_qkv.shape)
     (
-        sum_qkv,
         sum_qv_bias,
-        sum_out_proj,
         sum_out_bias,
-        sum_up,
         sum_up_bias,
-        sum_down,
         sum_down_bias,
         sum_gain,
         sum_shift,
-        embed_sum,
         sum_embed_bias,
         band_grad_sum,
         band_cross_sum,
-    ) = lax.psum(
-        (
-            grad_qkv,
-            grad_qv_bias,
-            grad_out_proj,
-            grad_out_bias,
-            grad_up,
-            grad_up_bias,
-            grad_down,
-            grad_down_bias,
-            grad_norm_gain,
-            grad_norm_bias,
-            embed_part,
-            grad_embed_bias,
-            band_grad,
-            band_cross,
-        ),
-        "dp",
-    )
+    ) = small
     pixel_grad = band_rstd[:, None] * (
         grad_pixel_hat
         - pixel_mask * (band_grad_sum[:, None] + band_cross_sum[:, None] * pixel_hat) / band_count
@@ -276,6 +569,7 @@
 
 
 def solution(mesh):
+    fast = dict(mesh.shape) == {"dp": 16, "tensor": 2}
     in_specs = (
         P("dp", None, None),
         P("dp"),
@@ -312,5 +606,5 @@
         P(),
     )
     return jax.shard_map(
-        per_device, mesh=mesh, in_specs=in_specs, out_specs=out_specs, check_vma=False
-    )
+        functools.partial(per_device, fast), mesh=mesh, in_specs=in_specs, out_specs=out_specs, check_vma=False
+    )

time: 897 us -> 562 us (0.63)
  waiting for transfers between devices: 599 us -> 110 us
  Pallas kernels: 0 us -> 286 us
  blocking collectives: 101 us -> 0 us
  between operations: 15.5 us -> 1.83 us
  other arithmetic: 40.2 us -> 28.4 us
    psum x4 -> x0, waiting for transfers between devices: 599 us -> none  [the longest x1 408 us: per_device(): lax.psum((grad_qkv, grad_qv_bias, grad_out_proj, grad_out_bias, grad_up,...]
    pallas_call x0 -> x2, Pallas kernels: none -> 286 us  [the longest x1 271 us: dp_sum(): pl.pallas_call(functools.partial(dp_kernel, shapes, R, K, delays), out_sh...]
    ppermute x0 -> x4, waiting for transfers between devices: none -> 110 us  [tensor_sum(): return part + lax.ppermute(part, 'tensor', [(0, 1), (1, 0)])]
    psum x2 -> x0, blocking collectives: 101 us -> none  [the longest x1 65.1 us: per_device(): lax.psum((grad_qkv, grad_qv_bias, grad_out_proj, grad_out_bias, grad_up,...]
    unnamed x108 -> x118, local copies, waits for them, and re-layouts: 31.7 us -> 34.5 us
  transfers between devices with their start and end apart: 4 -> 4, of which waited for: 4 -> 3; matrix products, arithmetic and copies ran while one was open for 5% -> 7% of each run, Pallas kernels for 0% -> 49%
where the time goes in v1:
time: 562 us; the launch traced here: 555 us
  Pallas kernels  286 us (51%)
  waiting for transfers between devices  110 us (20%)
  matrix products  63.5 us (11%)
  local copies, waits for them, and re-layouts  59.9 us (11%)
  other arithmetic  28.4 us (5%)
  starting transfers between devices  6.25 us (1%)
    pallas_call x1, Pallas kernels, dp_sum(): pl.pallas_call(functools.partial(dp_kernel, shapes, R, K, delays), out_sh...  271 us
    ppermute x4, waiting for transfers between devices, tensor_sum(): return part + lax.ppermute(part, 'tensor', [(0, 1), (1, 0)])  110 us
    unnamed x118, local copies, waits for them, and re-layouts  34.5 us
    dot_general x7, matrix products, contract_rows(): lax.dot_general(left_side, right_side, (((0,), (0,)), ((), ())), preferre...  19.8 us
    pallas_call x1, Pallas kernels, band_stats(): pl.pallas_call(functools.partial(stats_kernel, ranks, width // 3), out_sh...  15.1 us
    dot_general x1, matrix products, per_device(): jnp.dot(mlp_input, up_w, preferred_element_type=jnp.float32) + up_bias  13.1 us
    dot_general x7, matrix products, contract_cols(): lax.dot_general(left_side, right_side, (((1,), (1,)), ((), ())), preferre...  12.8 us
  transfers between devices with their start and end apart: 4, of which 3 were waited for; matrix products, arithmetic and copies ran while one was open for 7% of the time, Pallas kernels for 49%

profile of v1, /device:TPU:0, one launch (start us, length us, event | category | flops | bytes accessed | tf_op | source)
XLA Modules:
  0.0 555.5 jit_solution(6845057230162482671)
XLA Ops:
  0.7 0.8 convert_multiply_fusion
  3.7 0.8 fusion.70
  4.5 0.8 fusion.71
  5.3 15.1 %band_stats.1 = f32[8,768]{1,0:T(8,128)} custom-call(s32[2]{0:T(128)} %lens.1, bf16[2,256,768]{2,1,0:T(8,128)(2,1)} %pix.1), custom_call_target="tpu_custom_call" | custom-call | tf_op jit(solution)/shard_map/band_stats/pallas_call | solution.py:274
  20.3 0.8 slice_reduce_fusion.1
  21.6 1.3 fusion.24
  22.9 3.7 multiply_sine_fusion.1
  26.6 1.1 fusion.73
  29.1 1.3 copy-done.29
  30.4 1.5 convolution_convert_fusion.1
  32.6 1.5 fusion.25
  34.1 2.6 reshape.282
  36.8 2.5 copy.74
  39.3 1.5 reshape.283
  40.8 1.7 copy.72
  42.5 2.6 reshape.284
  45.1 2.5 copy.73
  47.6 2.1 fusion.74
  50.2 1.4 copy-done.6
  51.7 0.9 fusion.35
  54.5 1.6 collective-permute-start
  56.4 45.8 %collective-permute-done = f32[512,1024]{1,0:T(8,128)S(1)} collective-permute-done((f32[512,1024]{1,0:T(8,128)S(1)}, f32[512,1024]{1,0:T(8,128)S(1)}, u32[]{:S(2)}, u32[]{:S(2)}) %collective-permute-start) | collective-permute-done | bytes 2097184 | tf_op jit(solution)/shard_map/ppermute | solution.py:339
  102.9 2.2 copy-done.37
  105.1 13.1 %fusion.2 = (bf16[512,2048]{1,0:T(8,128)(2,1)}, f32[512,2048]{1,0:T(8,128)S(1)}) fusion(f32[2048]{0:T(1024)S(1)} %copy-done.40, bf16[1024,2048]{1,0:T(8,128)(2,1)S(1)} %copy-done.37, f32[512,1024]{1,0:T(8,128)S(1)} %get-tuple-element.47, f32[1024]{0:T(1024)S(1)} %bitcast.205, f32[1024]{0:T(1024)S(1)} %bitcast.184, f32[512]{0:T(512)S(1)} %add_rsqrt_fusion, ...), kind=kOutput, calls=%fused_computation.5 | convolution fusion | flops 2219311104 | bytes 12603392 | tf_op jit(solution)/shard_map/dot_general | solution.py:435
  118.2 4.0 convert_reduce_fusion
  122.2 2.4 fusion.77
  124.6 1.6 collective-permute-start.1
  126.2 1.3 slice.104
  127.7 6.0 %fusion.64.refs_2_ = f32[1024,2048]{1,0:T(8,128)} fusion(bf16[512,2048]{1,0:T(8,128)(2,1)S(1)} %get-tuple-element.87, f32[512,1024]{1,0:T(8,128)S(1)} %get-tuple-element.47, f32[1024]{0:T(1024)S(1)} %bitcast.206, f32[1024]{0:T(1024)S(1)} %bitcast.185, f32[512]{0:T(512)S(1)} %add_rsqrt_fusion, f32[512]{0:T(512)S(1)} %broadcast_multiply_fusion.4), kind=kOutput, calls=%fused_computation.143 | convolution fusion | flops 2150105088 | bytes 12595200 | tf_op jit(solution)/shard_map/dot_general | solution.py:303
  133.7 37.7 %collective-permute-done.1 = f32[512,1024]{1,0:T(8,128)S(1)} collective-permute-done((f32[512,1024]{1,0:T(8,128)S(1)}, f32[512,1024]{1,0:T(8,128)S(1)}, u32[]{:S(2)}, u32[]{:S(2)}) %collective-permute-start.1) | collective-permute-done | bytes 2097184 | tf_op jit(solution)/shard_map/ppermute | solution.py:339
  171.4 1.2 multiply_reduce_fusion.1
  172.6 0.9 fusion.67
  173.5 1.3 copy-done.13
  175.6 1.5 reshape.285
  177.1 1.7 copy.78
  178.8 3.2 convert_reduce_fusion.1
  182.4 1.0 multiply_reduce_fusion
  183.4 1.0 multiply_convert_fusion
  188.2 0.8 copy-done.30
  190.6 2.1 add_add_fusion
  192.6 1.5 collective-permute-start.2
  194.2 5.8 %fusion.78.refs_3_ = f32[2048,1024]{1,0:T(8,128)} fusion(bf16[512,2048]{1,0:T(8,128)(2,1)S(1)} %copy-done.42, bf16[512,1024]{1,0:T(8,128)(2,1)S(1)} %copy-done.34), kind=kOutput, calls=%fused_computation.157 | convolution fusion | flops 2147483648 | bytes 11534336 | tf_op jit(solution)/shard_map/dot_general | solution.py:303
  200.0 3.7 fusion.76
  203.9 1.9 convolution_bitcast_fusion
  207.3 3.4 pad_maximum_fusion
  210.7 2.0 fusion.57.refs_1_
  212.8 26.1 %collective-permute-done.2 = f32[512,1024]{1,0:T(8,128)} collective-permute-done((f32[512,1024]{1,0:T(8,128)}, f32[512,1024]{1,0:T(8,128)}, u32[]{:S(2)}, u32[]{:S(2)}) %collective-permute-start.2) | collective-permute-done | bytes 2097184 | tf_op jit(solution)/shard_map/ppermute | solution.py:339
  238.8 3.4 multiply_reduce_fusion.2
  242.4 1.6 collective-permute-start.3
  244.7 2.2 multiply_reduce_fusion.10
  247.3 2.6 fusion.53.refs_4_
  249.9 271.0 %dp_sum.1 = (f32[3072,512]{1,0:T(8,128)}, f32[512,1024]{1,0:T(8,128)S(1)}, f32[1024,2048]{1,0:T(8,128)}, f32[2048,1024]{1,0:T(8,128)}, f32[768,1024]{1,0:T(8,128)S(1)}, /*index=5*/f32[128,512]{1,0:T(8,128)S(1)}) custom-call(f32[3072,512]{1,0:T(8,128)} %bitcast.160, f32[512,1024]{1,0:T(8,128)S(1)} %copy-done.1, f32[1024,2048]{1,0:T(8,128)} %fusion.64.refs_2_, ...), custom_call_target="tpu_custom_call" | custom-call | tf_op jit(solution)/shard_map/dp_sum/pallas_call | solution.py:209
  521.0 1.7 copy-done.2
  522.6 1.3 copy-done.4
  528.5 3.8 subtract_multiply_fusion.2
  532.3 3.7 multiply_convert_fusion.1
  536.0 1.7 copy.127
  537.7 2.2 copy-done.17
  540.0 3.2 copy.128
  543.8 1.3 copy.129
  545.2 1.1 slice-done.3
  546.3 4.2 copy.130
  550.5 1.2 slice-done.1
  551.6 3.4 copy.131
  (166 shorter events, 23.0 us)
Async XLA Ops:
  0.6 26.0 %copy-start = (bf16[768,1024]{1,0:T(8,128)(2,1)S(1)}, bf16[768,1024]{1,0:T(8,128)(2,1)}, u32[]{:S(2)}) copy-start(bf16[768,1024]{1,0:T(8,128)(2,1)} %param.21) | copy-start | bytes 4718596
  5.3 21.4 %copy-start.41 = (f32[1024]{0:T(1024)S(1)}, f32[1024]{0:T(1024)}, u32[]{:S(2)}) copy-start(f32[1024]{0:T(1024)} %param.22) | copy-start | bytes 12292
  22.9 4.9 copy-start.26
  27.8 1.3 copy-start.8
  28.1 2.3 copy-start.29
  42.5 7.1 %copy-start.22 = (bf16[2,256,8,64]{1,3,2,0:T(8,128)(2,1)}, bf16[2,256,8,64]{1,3,2,0:T(8,128)(2,1)S(1)}, u32[]{:S(2)}) copy-start(bf16[2,256,8,64]{1,3,2,0:T(8,128)(2,1)S(1)} %copy.72) | copy-start | bytes 1572868
  49.6 2.0 copy-start.6
  49.6 2.0 copy-start.31
  52.5 1.2 copy-start.27
  53.2 3.2 copy-start.18
  53.2 2.9 copy-start.15
  53.7 48.4 %copy-start.9 = (f32[512,1024]{1,0:T(8,128)S(1)}, f32[512,1024]{1,0:T(8,128)}, u32[]{:S(2)}) copy-start(f32[512,1024]{1,0:T(8,128)} %copy-done.8) | copy-start | bytes 6291460
  53.7 48.4 %copy-start.35 = (f32[1024]{0:T(1024)S(1)}, f32[1024]{0:T(1024)}, u32[]{:S(2)}) copy-start(f32[1024]{0:T(1024)} %param.28) | copy-start | bytes 12292
  54.5 47.7 %collective-permute-start = (f32[512,1024]{1,0:T(8,128)S(1)}, f32[512,1024]{1,0:T(8,128)S(1)}, u32[]{:S(2)}, u32[]{:S(2)}) collective-permute-start(f32[512,1024]{1,0:T(8,128)S(1)} %fusion.75), channel_id=1, source_target_pairs={{0,1},{1,0},{2,3},{3,2},{4,5},{5,4},{6,7},{7,6},{8,9},{9,8},{10,11... | collective-permute-start | bytes 6291464 | tf_op jit(solution)/shard_map/ppermute | solution.py:339
  56.3 61.9 %copy-start.33 = (bf16[512,1024]{1,0:T(8,128)(2,1)}, bf16[512,1024]{1,0:T(8,128)(2,1)S(1)}, u32[]{:S(2)}) copy-start(bf16[512,1024]{1,0:T(8,128)(2,1)S(1)} %fusion.22) | copy-start | bytes 3145732
  102.2 2.9 copy-start.37
  102.5 70.0 %copy-start.11 = (f32[512,1024]{1,0:T(8,128)}, f32[512,1024]{1,0:T(8,128)S(1)}, u32[]{:S(2)}) copy-start(f32[512,1024]{1,0:T(8,128)S(1)} %get-tuple-element.47) | copy-start | bytes 6291460
  102.6 2.6 copy-start.40
  105.1 13.1 %copy-start.38 = (bf16[2048,1024]{1,0:T(8,128)(2,1)S(1)}, bf16[2048,1024]{1,0:T(8,128)(2,1)}, u32[]{:S(2)}) copy-start(bf16[2048,1024]{1,0:T(8,128)(2,1)} %param.31) | copy-start | bytes 12582916
  124.6 46.8 %collective-permute-start.1 = (f32[512,1024]{1,0:T(8,128)S(1)}, f32[512,1024]{1,0:T(8,128)S(1)}, u32[]{:S(2)}, u32[]{:S(2)}) collective-permute-start(f32[512,1024]{1,0:T(8,128)S(1)} %fusion.77), channel_id=1, source_target_pairs={{0,1},{1,0},{2,3},{3,2},{4,5},{5,4},{6,7},{7,6},{8,9},{9,8},{10,11... | collective-permute-start | bytes 6291464 | tf_op jit(solution)/shard_map/ppermute | solution.py:339
  173.5 1.4 copy-start.13
  178.8 3.5 copy-start.7
  178.8 3.6 copy-start.32
  183.4 1.0 copy-start.23
  184.4 1.0 copy-start.24
  186.9 3.6 copy-start.25
  186.9 2.1 copy-start.30
  188.2 2.3 copy-start.20
  190.6 3.6 copy-start.34
  190.6 3.6 copy-start.42
  192.6 46.2 %collective-permute-start.2 = (f32[512,1024]{1,0:T(8,128)}, f32[512,1024]{1,0:T(8,128)}, u32[]{:S(2)}, u32[]{:S(2)}) collective-permute-start(f32[512,1024]{1,0:T(8,128)} %add_add_fusion), channel_id=1, source_target_pairs={{0,1},{1,0},{2,3},{3,2},{4,5},{5,4},{6,7},{7,6},{8,9},{9,8},{10,11... | collective-permute-start | bytes 6291464 | tf_op jit(solution)/shard_map/ppermute | solution.py:339
  194.2 5.8 %copy-start.39 = (bf16[2048,1024]{1,0:T(8,128)(2,1)S(1)}, bf16[2048,1024]{1,0:T(8,128)(2,1)}, u32[]{:S(2)}) copy-start(bf16[2048,1024]{1,0:T(8,128)(2,1)} %param.31) | copy-start | bytes 12582916
  203.9 1.9 copy-start.21
  207.3 3.5 copy-start.14
  207.3 3.5 copy-start.19
  210.7 28.1 %copy-start.10 = (f32[512,1024]{1,0:T(8,128)S(1)}, f32[512,1024]{1,0:T(8,128)}, u32[]{:S(2)}) copy-start(f32[512,1024]{1,0:T(8,128)} %copy-done.8) | copy-start | bytes 6291460
  242.3 2.3 copy-start.16
  242.4 290.0 %collective-permute-start.3 = (f32[512,1024]{1,0:T(8,128)}, f32[512,1024]{1,0:T(8,128)}, u32[]{:S(2)}, u32[]{:S(2)}) collective-permute-start(f32[512,1024]{1,0:T(8,128)} %fusion.76), channel_id=1, source_target_pairs={{0,1},{1,0},{2,3},{3,2},{4,5},{5,4},{6,7},{7,6},{8,9},{9,8},{10,11... | collective-permute-start | bytes 6291464 | tf_op jit(solution)/shard_map/ppermute | solution.py:339
  244.7 2.2 copy-start.28
  247.3 2.6 copy-start.1
  520.9 1.7 copy-start.2
  522.6 1.3 copy-start.4
  528.2 4.1 copy-start.36
  528.5 3.9 copy-start.12
  532.3 3.7 copy-start.3
  536.0 3.9 copy-start.17
  536.0 9.1 %slice-start.2 = ((s8[8388608]{0:T(1024)(128)(4,1)}), s8[4194304]{0:T(1024)(128)(4,1)S(1)}, s32[]{:S(2)}) async-start(s8[8388608]{0:T(1024)(128)(4,1)} %bitcast.163), calls=%async_computation.2 | async-start | bytes 8388608
  539.9 3.9 copy-start.5
  540.0 6.3 %slice-start.3 = ((s8[8388608]{0:T(1024)(128)(4,1)}), s8[4194304]{0:T(1024)(128)(4,1)S(1)}, s32[]{:S(2)}) async-start(s8[8388608]{0:T(1024)(128)(4,1)} %bitcast.163), calls=%async_computation.3 | async-start | bytes 8388608
  543.8 6.6 %slice-start = ((s8[8388608]{0:T(1024)(128)(4,1)}), s8[4194304]{0:T(1024)(128)(4,1)S(1)}, s32[]{:S(2)}) async-start(s8[8388608]{0:T(1024)(128)(4,1)} %bitcast.161), calls=%async_computation | async-start | bytes 8388608
  546.3 5.4 slice-start.1

commit v2 on v1

--- a/solution.py
+++ b/solution.py
@@ -14,12 +14,26 @@
 W = 512
 
 
-SEND = ("c","x","oa","ob","ja","jb","xb","ga","gb","na","fa","nb","fb","xg","cg")
-
-def dp_kernel(shapes, R, K, delays, *refs):
+SEND = (
+    "c","x","oa","ob","ja","jb","xb","ga","gb","na","fa","nb","fb","xg","cg")
+
+FETCH = 17
+
+
+def back_kernel(shapes, R, K, delays, *refs):
     n = len(shapes)
-    ins, outs = refs[:n], refs[n:2*n]
-    own, cl, xl, ab, oa, ob, ja, jb, nbuf, xbl, fin, ssem, rsem, lsem = refs[2*n:]
+    (lens, up_in, down_in, part_in, mlp_in, pre_in), fetched = refs[:6], refs[6 : 6 + FETCH]
+    outs = refs[6 + FETCH : 6 + FETCH + n]
+    mlp_out, pixel_out = refs[6 + FETCH + n : 8 + FETCH + n]
+    scratch = refs[8 + FETCH + n :]
+    held, scratch = scratch[:FETCH], scratch[FETCH:]
+    (part, normed_two, inv_two, grad_two, attended, out_w, queries, keys, values, attn_in, qkv_w,
+     normed_one, inv_one, pixel_low, pixel_hat, embed_w, gains) = held
+    (land, land_two, back_part, grad_one, one_low, zero_low, grad_att, grad_proj, grad_pix, sums,
+     out_grad, qkv_grad, embed_grad, small_grad) = scratch[:14]
+    own, cl, xl, ab, oa, ob, ja, jb, nbuf, xbl, fin, ssem, rsem, lsem, fsem, ysend, yrecv = scratch[14:]
+    ins = (up_in, down_in, out_grad, qkv_grad, embed_grad, small_grad)
+    slots = normed_one.shape[0] // 2
     H, Q, E = R//2, R//4, R//8
     i = lax.axis_index("dp"); t = lax.axis_index("tensor")
     c = lax.rem(i, 2); x = lax.rem(i//2, 2); z = i//4
@@ -31,21 +45,156 @@
     dev_x = (z*4 + (1-x)*2 + c, t)
     dev_o = ((side*2 + 1 - pos)*4 + x*2 + c, t)
     dev_j = ((3 - z)*4 + x*2 + c, t)
+    dev_y = (i, 1 - t)
+    fetches = [pltpu.make_async_copy(fetched[q], held[q], fsem.at[q]) for q in range(FETCH)]
+    fetches.append(pltpu.make_async_copy(pre_in, small_grad.at[pl.ds(0, 8)], fsem.at[FETCH]))
+    for q in fetches:
+        q.start()
     bar = pltpu.get_barrier_semaphore()
-    for d in (dev_c, dev_x, dev_o):
+    for d in (dev_c, dev_x, dev_o, dev_y):
         pl.semaphore_signal(bar, inc=1, device_id=d, device_id_type=MESH)
     @pl.when(inner)
     def _():
         pl.semaphore_signal(bar, inc=1, device_id=dev_j, device_id_type=MESH)
-        pl.semaphore_wait(bar, 4)
+        pl.semaphore_wait(bar, 5)
     @pl.when(outer)
     def _():
-        pl.semaphore_wait(bar, 3)
+        pl.semaphore_wait(bar, 4)
+    def al(v, m): return pl.multiple_of(v, m)
+
+    def across(q, src, dst):
+        return pltpu.make_async_remote_copy(
+            src_ref=src, dst_ref=dst, send_sem=ysend.at[q], recv_sem=yrecv.at[q],
+            device_id=dev_y, device_id_type=MESH)
+
+    first_sum = across(0, part_in, land)
+    second_sum = across(1, back_part, land_two)
+    third_sum = across(2, mlp_in, mlp_out)
+    pixel_copy = pltpu.make_async_copy(grad_pix, pixel_out, fsem.at[FETCH + 1])
+    first_sum.start()
+    sums[...] = jnp.zeros_like(sums)
+    small_grad[pl.ds(8, 120), :] = jnp.zeros((120, W), jnp.float32)
+    f32, bf16 = jnp.float32, jnp.bfloat16
+
+    def mm(a, b, ca, cb):
+        return lax.dot_general(a, b, (((ca,), (cb,)), ((), ())), preferred_element_type=f32)
+
+    def add_sum(row, value):
+        width = value.shape[1]
+        sums[row : row + 1, :width] = sums[row : row + 1, :width] + jnp.sum(value, axis=0, keepdims=True)
+
+    def norm_back(upstream, normed, inverse, gain_row):
+        scaled = upstream * gain_row
+        return inverse * (
+            scaled
+            - jnp.mean(scaled, axis=-1, keepdims=True)
+            - normed * jnp.mean(scaled * normed, axis=-1, keepdims=True))
+
+    def second_norm(q):
+        rows = pl.ds(al(q * 64, 64), 64)
+        upstream, normed = part[rows, :] + land[rows, :], normed_two[rows, :]
+        grad = grad_two[rows, :] + norm_back(upstream, normed, inv_two[rows, 0:1], gains[1:2, :])
+        grad_one[rows, :] = grad
+        one_low[rows, :] = grad.astype(bf16)
+        add_sum(0, grad)
+        add_sum(1, upstream * normed)
+        add_sum(2, upstream)
+
+    def into_heads(q):
+        rows = pl.ds(al(q * 128, 128), 128)
+        grad_att[rows, :] = mm(one_low[rows, :], out_w[...], 1, 1).astype(bf16)
+
+    def attention(q):
+        image, pair = q // 4, lax.rem(q, 4)
+        rows, cols = pl.ds(al(image * slots, slots), slots), pl.ds(al(pair * 128, 128), 128)
+        qs, ks, vs, gs = queries[rows, cols], keys[rows, cols], values[rows, cols], grad_att[rows, cols]
+        keep = lax.broadcasted_iota(jnp.int32, (1, slots), 1) < lens[image]
+        scale = 1.0 / math.sqrt(HD)
+        dq, dk, dv = [], [], []
+        for h in range(2):
+            part_of = slice(h * HD, (h + 1) * HD)
+            qh, kh, vh, gh = qs[:, part_of], ks[:, part_of], vs[:, part_of], gs[:, part_of]
+            scores = jnp.where(keep, mm(qh, kh, 1, 1) * scale, -1e30)
+            exps = jnp.exp(scores - jnp.max(scores, axis=-1, keepdims=True))
+            probs = exps / jnp.sum(exps, axis=-1, keepdims=True)
+            grad_probs = mm(gh, vh, 1, 1)
+            dv.append(mm(probs.astype(bf16), gh, 0, 0))
+            dot = jnp.sum(probs * grad_probs, axis=-1, keepdims=True)
+            grad_scores = (probs * (grad_probs - dot)).astype(bf16)
+            dq.append(mm(grad_scores, kh, 1, 0) * scale)
+            dk.append(mm(grad_scores, qh, 0, 0) * scale)
+        for at, pieces in enumerate((dq, dk, dv)):
+            grad_proj[at, rows, cols] = jnp.concatenate(pieces, axis=1).astype(bf16)
+
+    def into_norm(q):
+        rows = pl.ds(al(q * 128, 128), 128)
+        back_part[rows, :] = (
+            mm(grad_proj[0, rows, :], qkv_w[0], 1, 1)
+            + mm(grad_proj[1, rows, :], qkv_w[1], 1, 1)
+            + mm(grad_proj[2, rows, :], qkv_w[2], 1, 1))
+
+    def out_weight(q):
+        cols = pl.ds(al(q * 128, 128), 128)
+        out_grad[cols, :] = mm(attended[:, cols], one_low[...], 0, 0)
+
+    def proj_weight(q):
+        which, block = q // 4, lax.rem(q, 4)
+        cols = pl.ds(al(block * 256, 256), 256)
+        qkv_grad[pl.ds(al(q * 256, 256), 256), :] = mm(attn_in[:, cols], grad_proj[which], 0, 0)
+
+    def first_norm(q):
+        rows = pl.ds(al(q * 64, 64), 64)
+        upstream, normed = back_part[rows, :] + land_two[rows, :], normed_one[rows, :]
+        grad = grad_one[rows, :] + norm_back(upstream, normed, inv_one[rows, 0:1], gains[0:1, :])
+        zero_low[rows, :] = grad.astype(bf16)
+        add_sum(3, upstream * normed)
+        add_sum(4, upstream)
+        add_sum(5, grad)
+
+    def embed_weight(q):
+        cols = pl.ds(al(q * 256, 256), 256)
+        embed_grad[cols, :] = mm(pixel_low[:, cols], zero_low[...], 0, 0)
+
+    def pixels_back(q):
+        rows = pl.ds(al(q * 128, 128), 128)
+        grad = mm(zero_low[rows, :], embed_w[...], 1, 1)
+        grad_pix[rows, :] = grad
+        add_sum(6, grad)
+        add_sum(7, grad * pixel_hat[rows, :])
+
+    def pack(q):
+        for row in range(8):
+            small_grad[8 + 2 * row : 9 + 2 * row, :] = sums[row : row + 1, :W]
+            small_grad[9 + 2 * row : 10 + 2 * row, :] = sums[row : row + 1, W:]
+        for row, at in ((24, 0), (25, 2)):
+            small_grad[row : row + 1, :] = jnp.sum(grad_proj[at].astype(f32), axis=0, keepdims=True)
+
+    def fetch_wait(q):
+        for one in fetches:
+            one.wait()
+
+    def first_wait(q):
+        first_sum.wait()
+
+    def second_start(q):
+        second_sum.start()
+
+    def second_wait(q):
+        second_sum.wait()
+        third_sum.start()
+
+    def pixel_start(q):
+        pixel_copy.start()
+
+    plan = (
+        (12, 1, fetch_wait), (23, 1, first_wait), (24, 8, second_norm), (32, 4, into_heads),
+        (36, 8, attention), (44, 4, into_norm), (48, 1, second_start), (49, 4, out_weight),
+        (53, 12, proj_weight), (71, 1, second_wait), (72, 8, first_norm), (80, 3, embed_weight),
+        (83, 4, pixels_back), (87, 1, pack), (88, 1, pixel_start))
     starts, total = [], 0
     for (rows, cols) in shapes:
         starts.append(total); total += (rows//(2*R))*(cols//W)
     NC = total
-    def al(v, m): return pl.multiple_of(v, m)
     def slot(j): return lax.rem(j, K)
     a_mine = al(x*Q, Q); a_other = al((1-x)*Q, Q)
     e_near = al(side*E, E); e_far = al((1-side)*E, E)
@@ -197,24 +346,50 @@
                 pltpu.make_async_copy(hbm(ins[a], a, j, c), own.at[s], lsem.at[0, s]).start()
                 rc("c", hbm(ins[a], a, j, 1 - c), cl.at[s], dev_c, s).start()
             each(j, f)
+        for begin, number, piece in plan:
+            if number == 1:
+                pl.when(tt == begin)(functools.partial(piece, 0))
+            else:
+                pl.when((tt >= begin) & (tt < begin + number))(functools.partial(piece, tt - begin))
         return carry
     lax.fori_loop(0, NC + d[7], step, 0)
-
-def dp_sum(arrays, R=64, K=16, delays=(0,1,3,5,7,9,12,13,1), name="dp_sum", cid=1):
-    shapes = tuple(a.shape for a in arrays)
-    n = len(arrays)
-    H, Q, E = R//2, R//4, R//8
-    f32 = jnp.float32
+    third_sum.wait()
+    pixel_copy.wait()
+
+
+def back_pass(lengths, grad_up, grad_down, part, mlp_part, pre, fetched, R=64, K=14,
+              delays=(0, 1, 3, 5, 7, 9, 12, 13, 1)):
+    f32, bf16 = jnp.float32, jnp.bfloat16
+    tokens, width = part.shape
+    local = grad_up.shape[0] // 2
+    patch = fetched[13].shape[1]
+    shapes = (grad_up.shape, grad_down.shape, (local, width), (3 * width, local), (patch, width), (2 * R, W))
+    n = len(shapes)
+    H, Q, E = R // 2, R // 4, R // 8
     V = lambda r: pltpu.VMEM((K, r, W), f32)
+    anywhere = pl.BlockSpec(memory_space=pl.ANY)
+    held = [pltpu.VMEM(a.shape, a.dtype) for a in fetched]
+    out = [jax.ShapeDtypeStruct(s, f32) for s in shapes]
+    out += [jax.ShapeDtypeStruct((tokens, width), f32), jax.ShapeDtypeStruct((tokens, patch), f32)]
     return pl.pallas_call(
-        functools.partial(dp_kernel, shapes, R, K, delays),
-        out_shape=[jax.ShapeDtypeStruct(s, f32) for s in shapes],
-        in_specs=[pl.BlockSpec(memory_space=pl.ANY)]*n,
-        out_specs=[pl.BlockSpec(memory_space=pl.ANY)]*n,
-        scratch_shapes=[V(R), V(R), V(Q), V(Q), V(Q), V(H), V(E), V(Q), V(Q), V(Q), V(R),
-            pltpu.SemaphoreType.DMA((len(SEND), K)), pltpu.SemaphoreType.DMA((len(SEND), K)), pltpu.SemaphoreType.DMA((2, K))],
-        compiler_params=pltpu.CompilerParams(collective_id=cid, has_side_effects=True, vmem_limit_bytes=40 << 20),
-        name=name)(*arrays)
+        functools.partial(back_kernel, shapes, R, K, delays),
+        out_shape=out,
+        in_specs=[pl.BlockSpec(memory_space=pltpu.SMEM)] + [anywhere] * (5 + FETCH),
+        out_specs=[anywhere] * len(out),
+        scratch_shapes=[
+            *held,
+            pltpu.VMEM((tokens, width), f32), pltpu.VMEM((tokens, width), f32), pltpu.VMEM((tokens, width), f32),
+            pltpu.VMEM((tokens, width), f32), pltpu.VMEM((tokens, width), bf16), pltpu.VMEM((tokens, width), bf16),
+            pltpu.VMEM((tokens, local), bf16), pltpu.VMEM((3, tokens, local), bf16),
+            pltpu.VMEM((tokens, patch), f32), pltpu.VMEM((8, width), f32),
+            pltpu.VMEM(shapes[2], f32), pltpu.VMEM(shapes[3], f32), pltpu.VMEM(shapes[4], f32), pltpu.VMEM(shapes[5], f32),
+            V(R), V(R), V(Q), V(Q), V(Q), V(H), V(E), V(Q), V(Q), V(Q), V(R),
+            pltpu.SemaphoreType.DMA((len(SEND), K)), pltpu.SemaphoreType.DMA((len(SEND), K)),
+            pltpu.SemaphoreType.DMA((2, K)), pltpu.SemaphoreType.DMA((FETCH + 2,)),
+            pltpu.SemaphoreType.DMA((3,)), pltpu.SemaphoreType.DMA((3,)),
+        ],
+        compiler_params=pltpu.CompilerParams(collective_id=1, has_side_effects=True, vmem_limit_bytes=66_000_000),
+        name="back_pass")(lengths, grad_up, grad_down, part, mlp_part, pre, *fetched)
 
 
 def stats_kernel(ranks, band_width, lens, pix, out, mine, table, ssem, rsem):
@@ -445,6 +620,42 @@
     )
     grad_up = contract_rows(mlp_input, grad_hidden)
     grad_up_bias = jnp.sum(grad_hidden.astype(jnp.float32), axis=0)
+    if fast:
+        spread = lambda column: jnp.broadcast_to(column, (tokens, 128))
+        pre = jnp.concatenate([grad_up_bias, jnp.sum(grad_two, axis=0), jnp.zeros((1024,), jnp.float32)])
+        fetched = (
+            contract_cols(grad_hidden, up_w), normed_two, spread(inverse_two), grad_two, attended, out_w,
+            queries, key_rows, values, attn_input, qkv_w, normed_one, spread(inverse_one), pixel_low,
+            pixel_hat.reshape(tokens, patch_width), embed_w, norm_gain)
+        sum_up, sum_down, sum_out_proj, sum_qkv, embed_sum, small, mlp_other, grad_pixel_hat = back_pass(
+            lengths, grad_up, grad_down, fetched[0], mlp_part, pre.reshape(8, W), fetched)
+        flat = small.reshape(-1)
+        rows = small[8:24].reshape(8, 2 * W)
+        sum_up_bias, sum_down_bias = flat[:2048], flat[2048:3072]
+        band = rows[6:8, :patch_width].reshape(2, 3, band_width).sum(axis=-1)
+        stream_two = stream_one + (mlp_part + mlp_other) + down_bias
+        output = (stream_two * row_valid).astype(jnp.bfloat16).reshape(images, slot_count, model_width)
+        grad_pixel_hat = grad_pixel_hat.reshape(images, slot_count, 3, band_width)
+        pixel_grad = band_rstd[:, None] * (
+            grad_pixel_hat
+            - pixel_mask * (band[0][:, None] + band[1][:, None] * pixel_hat) / band_count
+        )
+        return (
+            output,
+            pixel_grad.reshape(images, slot_count, patch_width),
+            embed_sum,
+            rows[5],
+            jnp.stack([rows[3], rows[1]]),
+            jnp.stack([rows[4], rows[2]]),
+            sum_qkv.reshape(3, model_width, local_width),
+            small[24:26],
+            sum_out_proj,
+            rows[0],
+            sum_up,
+            sum_up_bias,
+            sum_down,
+            sum_down_bias,
+        )
     grad_mlp_in = tensor_sum(contract_cols(grad_hidden, up_w))
     grad_one = grad_two + normalize_back(grad_mlp_in, normed_two, inverse_two, norm_gain[1])
     grad_out_bias = jnp.sum(grad_one, axis=0)
@@ -521,17 +732,7 @@
         band_cross,
     )
     large = (grad_qkv.reshape(-1, local_width), grad_out_proj, grad_up, grad_down, embed_part)
-    if fast:
-        packed = jnp.concatenate([piece.reshape(-1) for piece in small])
-        packed = jnp.pad(packed, (0, 128 * W - packed.shape[0])).reshape(128, W)
-        *large, packed = dp_sum((*large, packed))
-        flat, at, pieces = packed.reshape(-1), 0, []
-        for piece in small:
-            pieces.append(flat[at : at + piece.size].reshape(piece.shape))
-            at += piece.size
-        small = pieces
-    else:
-        large, small = lax.psum((large, small), "dp")
+    large, small = lax.psum((large, small), "dp")
     sum_qkv, sum_out_proj, sum_up, sum_down, embed_sum = large
     sum_qkv = sum_qkv.reshape(grad_qkv.shape)
     (

time: 562 us -> 460 us (0.82)
  waiting for transfers between devices: 110 us -> 42.7 us
  matrix products: 63.5 us -> 44.7 us
  local copies, waits for them, and re-layouts: 59.9 us -> 42.7 us
  Pallas kernels: 286 us -> 293 us
    ppermute x4 -> x1, waiting for transfers between devices: 110 us -> 42.7 us  [tensor_sum(): return part + lax.ppermute(part, 'tensor', [(0, 1), (1, 0)])]
    dot_general x7 -> x2, matrix products: 19.8 us -> 11.6 us  [contract_rows(): lax.dot_general(left_side, right_side, (((0,), (0,)), ((), ())), preferre...]
    unnamed x118 -> x75, local copies, waits for them, and re-layouts: 34.5 us -> 26.9 us
    pallas_call x1, Pallas kernels: 271 us -> 278 us  [back_pass(): pl.pallas_call(functools.partial(back_kernel, shapes, R, K, delays), out_...]
    reduce_sum x8 -> x2, other arithmetic: 7.31 us -> 1.59 us  [the longest x1 1.5 us: per_device(): jnp.sum(grad_two, axis=0)]
    dot_general x7 -> x2, matrix products: 12.8 us -> 7.99 us  [contract_cols(): lax.dot_general(left_side, right_side, (((1,), (1,)), ((), ())), preferre...]
  transfers between devices with their start and end apart: 4 -> 1, of which waited for: 3 -> 1; matrix products, arithmetic and copies ran while one was open for 7% -> 1% of each run, Pallas kernels for 49% -> 0%
where the time goes in v2:
time: 460 us; the launch traced here: 451 us
  Pallas kernels  293 us (64%)
  matrix products  44.7 us (10%)
  local copies, waits for them, and re-layouts  42.7 us (9%)
  waiting for transfers between devices  42.7 us (9%)
  other arithmetic  25.7 us (6%)
    pallas_call x1, Pallas kernels, back_pass(): pl.pallas_call(functools.partial(back_kernel, shapes, R, K, delays), out_...  278 us
    ppermute x1, waiting for transfers between devices, tensor_sum(): return part + lax.ppermute(part, 'tensor', [(0, 1), (1, 0)])  42.7 us
    unnamed x75, local copies, waits for them, and re-layouts  26.9 us
    pallas_call x1, Pallas kernels, band_stats(): pl.pallas_call(functools.partial(stats_kernel, ranks, width // 3), out_sh...  15.1 us
    dot_general x2, matrix products, contract_rows(): lax.dot_general(left_side, right_side, (((0,), (0,)), ((), ())), preferre...  11.6 us
    dot_general x1, matrix products, per_device(): jnp.dot(mlp_input, up_w, preferred_element_type=jnp.float32) + up_bias  11.2 us
  transfers between devices with their start and end apart: 1, of which 1 were waited for; matrix products, arithmetic and copies ran while one was open for 1% of the time, Pallas kernels for 0%

profile of v2, /device:TPU:0, one launch (start us, length us, event | category | flops | bytes accessed | tf_op | source)
XLA Modules:
  0.0 451.4 jit_solution(5395441750543719742)
XLA Ops:
  0.7 0.8 convert_multiply_fusion
  1.5 0.8 multiply_bitcast_fusion
  2.2 0.8 fusion.52
  3.0 0.7 fusion.48
  3.7 0.8 fusion.51
  4.5 0.8 fusion.50
  5.3 15.1 %band_stats.1 = f32[8,768]{1,0:T(8,128)} custom-call(s32[2]{0:T(128)} %refs_0_.1, bf16[2,256,768]{2,1,0:T(8,128)(2,1)} %pix.1), custom_call_target="tpu_custom_call" | custom-call | tf_op jit(solution)/shard_map/band_stats/pallas_call | solution.py:449
  20.3 0.8 slice_reduce_fusion.1
  21.4 0.1 copy.57
  21.6 2.5 fusion.22
  24.0 3.7 multiply_sine_fusion.1
  27.8 1.1 fusion.53
  28.9 0.3 multiply_reduce_fusion.2
  29.3 1.9 add_convert_fusion.1
  31.2 1.5 copy-done.8
  32.7 1.5 convolution_convert_fusion.refs_13_
  34.2 1.5 fusion.24.refs_12_
  35.7 1.5 fusion.23.refs_14_
  37.2 1.6 reshape.215
  38.9 2.4 reshape.213
  41.3 2.4 reshape.214
  43.6 1.9 fusion.27
  45.6 1.6 fusion.54
  47.2 0.5 fusion.26
  47.8 0.5 copy.47
  48.5 2.0 fusion.55
  50.5 1.5 collective-permute-start
  52.0 1.2 slice.124
  53.2 1.0 copy.48.refs_10_
  54.2 1.5 multiply_reduce_fusion
  55.7 42.7 %collective-permute-done = f32[512,1024]{1,0:T(8,128)} collective-permute-done((f32[512,1024]{1,0:T(8,128)}, f32[512,1024]{1,0:T(8,128)}, u32[]{:S(2)}, u32[]{:S(2)}) %collective-permute-start) | collective-permute-done | bytes 2097184 | tf_op jit(solution)/shard_map/ppermute | solution.py:514
  98.4 3.2 fusion.49
  101.7 0.3 multiply_reduce_fusion.1
  102.0 0.3 subtract_multiply_fusion.refs_7_
  102.3 3.0 copy-done.17
  105.4 11.2 %fusion.3 = (bf16[512,2048]{1,0:T(8,128)(2,1)S(1)}, f32[512,2048]{1,0:T(8,128)S(1)}) fusion(f32[2048]{0:T(1024)S(1)} %copy-done.19, bf16[1024,2048]{1,0:T(8,128)(2,1)S(1)} %copy-done.17, f32[512,1024]{1,0:T(8,128)S(1)} %subtract_multiply_fusion.refs_7_, f32[1024]{0:T(1024)S(1)} %bitcast.118, f32[1024]{0:T(1024)S(1)} %bitcast.120), kind=kOutput, calls=%fused_computation.5 | convolution fusion | flops 2218262528 | bytes 12599296 | tf_op jit(solution)/shard_map/dot_general | solution.py:610
  116.6 4.3 convert_reduce_fusion
  120.9 3.7 fusion.57.refs_3_.refs_6_
  124.6 5.8 %fusion.40.refs_1_ = f32[1024,2048]{1,0:T(8,128)} fusion(bf16[512,2048]{1,0:T(8,128)(2,1)S(1)} %get-tuple-element.72, f32[512,1024]{1,0:T(8,128)S(1)} %subtract_multiply_fusion.refs_7_, f32[1024]{0:T(1024)S(1)} %bitcast.119, f32[1024]{0:T(1024)S(1)} %bitcast.121), kind=kOutput, calls=%fused_computation.74 | convolution fusion | flops 2149056512 | bytes 12591104 | tf_op jit(solution)/shard_map/dot_general | solution.py:478
  130.4 3.7 fusion.56.refs_4_
  134.1 5.8 %fusion.37.refs_2_ = f32[2048,1024]{1,0:T(8,128)} fusion(bf16[512,2048]{1,0:T(8,128)(2,1)S(1)} %get-tuple-element.69, f32[512,1024]{1,0:T(8,128)S(1)} %get-tuple-element.73.refs_9_), kind=kOutput, calls=%fused_computation.71 | convolution fusion | flops 2148007936 | bytes 12582912 | tf_op jit(solution)/shard_map/dot_general | solution.py:478
  140.0 0.6 reshape.206.refs_5_
  140.6 0.8 broadcast_in_dim.22.refs_18_
  141.4 0.8 broadcast_in_dim.17.refs_8_
  142.2 277.7 %back_pass.1 = (f32[1024,2048]{1,0:T(8,128)}, f32[2048,1024]{1,0:T(8,128)}, f32[512,1024]{1,0:T(8,128)}, f32[3072,512]{1,0:T(8,128)}, f32[768,1024]{1,0:T(8,128)...) custom-call(s32[2]{0:T(128)} %refs_0_.1, f32[1024,2048]{1,0:T(8,128)} %fusion.40.refs_1_, ...), custom_call_target="tpu_custom_call" | custom-call | tf_op jit(solution)/shard_map/back_pass/pallas_call | solution.py:374
  420.0 0.9 slice_bitcast_fusion
  420.8 0.8 slice.120
  421.6 1.5 slice_bitcast_fusion.1
  423.1 0.6 copy.68
  423.7 0.6 copy.69
  424.6 0.6 copy.67
  425.2 0.6 copy.62
  425.8 4.3 multiply_convert_fusion
  430.1 0.6 pad_maximum_fusion.2
  430.7 0.6 pad_maximum_fusion.1
  431.3 2.4 subtract_multiply_fusion.2
  433.7 1.7 copy.81
  435.4 3.2 copy.82
  438.6 1.4 copy-done.11
  440.0 1.3 copy.83
  441.3 0.6 slice-done.3
  441.9 4.3 copy.84
  446.2 1.4 slice-done.1
  447.6 3.4 copy.85
  (85 shorter events, 0.9 us)
Async XLA Ops:
  0.6 27.1 %copy-start.12 = (bf16[768,1024]{1,0:T(8,128)(2,1)S(1)}, bf16[768,1024]{1,0:T(8,128)(2,1)}, u32[]{:S(2)}) copy-start(bf16[768,1024]{1,0:T(8,128)(2,1)} %refs_21_.1) | copy-start | bytes 4718596
  0.7 27.1 %copy-start.20 = (f32[1024]{0:T(1024)S(1)}, f32[1024]{0:T(1024)}, u32[]{:S(2)}) copy-start(f32[1024]{0:T(1024)} %param.22) | copy-start | bytes 12292
  24.0 4.9 %copy-start.10 = (bf16[512,768]{1,0:T(8,128)(2,1)}, bf16[512,768]{1,0:T(8,128)(2,1)S(1)}, u32[]{:S(2)}) copy-start(bf16[512,768]{1,0:T(8,128)(2,1)S(1)} %get-tuple-element.37.refs_19_) | copy-start | bytes 2359300
  27.8 1.5 copy-start.7
  28.9 2.3 copy-start.2
  29.3 3.4 copy-start.8
  31.2 4.6 %copy-start.6 = (bf16[512,1024]{1,0:T(8,128)(2,1)}, bf16[512,1024]{1,0:T(8,128)(2,1)S(1)}, u32[]{:S(2)}) copy-start(bf16[512,1024]{1,0:T(8,128)(2,1)S(1)} %get-tuple-element.34.refs_15_) | copy-start | bytes 3145732
  31.2 102.9 %copy-start.1 = (f32[512,1024]{1,0:T(8,128)}, f32[512,1024]{1,0:T(8,128)S(1)}, u32[]{:S(2)}) copy-start(f32[512,1024]{1,0:T(8,128)S(1)} %get-tuple-element.73.refs_9_) | copy-start | bytes 6291460
  45.6 1.7 copy-start.14
  47.2 1.2 copy-start.5
  47.8 50.6 %copy-start.15 = (f32[1024]{0:T(1024)S(1)}, f32[1024]{0:T(1024)}, u32[]{:S(2)}) copy-start(f32[1024]{0:T(1024)} %param.28) | copy-start | bytes 12292
  50.5 47.9 %collective-permute-start = (f32[512,1024]{1,0:T(8,128)}, f32[512,1024]{1,0:T(8,128)}, u32[]{:S(2)}, u32[]{:S(2)}) collective-permute-start(f32[512,1024]{1,0:T(8,128)} %fusion.55), channel_id=1, source_target_pairs={{0,1},{1,0},{2,3},{3,2},{4,5},{5,4},{6,7},{7,6},{8,9},{9,8},{10,11... | collective-permute-start | bytes 6291464 | tf_op jit(solution)/shard_map/ppermute | solution.py:514
  101.6 15.0 %copy-start = (f32[512,1024]{1,0:T(8,128)}, f32[512,1024]{1,0:T(8,128)S(1)}, u32[]{:S(2)}) copy-start(f32[512,1024]{1,0:T(8,128)S(1)} %get-tuple-element.33) | copy-start | bytes 6291460
  101.7 3.7 copy-start.17
  101.7 3.7 copy-start.19
  102.3 22.3 %copy-start.3 = (f32[512,1024]{1,0:T(8,128)}, f32[512,1024]{1,0:T(8,128)S(1)}, u32[]{:S(2)}) copy-start(f32[512,1024]{1,0:T(8,128)S(1)} %subtract_multiply_fusion.refs_7_) | copy-start | bytes 6291460
  105.4 11.3 %copy-start.18 = (bf16[2048,1024]{1,0:T(8,128)(2,1)S(1)}, bf16[2048,1024]{1,0:T(8,128)(2,1)}, u32[]{:S(2)}) copy-start(bf16[2048,1024]{1,0:T(8,128)(2,1)} %param.31) | copy-start | bytes 12582916
  142.2 283.5 %copy-start.16 = (f32[1024]{0:T(1024)S(1)}, f32[1024]{0:T(1024)}, u32[]{:S(2)}) copy-start(f32[1024]{0:T(1024)} %param.32) | copy-start | bytes 12292
  419.9 11.4 %copy-start.4 = (bf16[2,256,768]{2,1,0:T(8,128)(2,1)S(1)}, bf16[2,256,768]{2,1,0:T(8,128)(2,1)}, u32[]{:S(2)}) copy-start(bf16[2,256,768]{2,1,0:T(8,128)(2,1)} %pix.1) | copy-start | bytes 2359300
  419.9 11.4 %copy-start.13 = (f32[512,768]{1,0:T(8,128)S(1)}, f32[512,768]{1,0:T(8,128)}, u32[]{:S(2)}) copy-start(f32[512,768]{1,0:T(8,128)} %get-tuple-element.23) | copy-start | bytes 4718596
  425.8 7.9 %copy-start.9 = (f32[768,1024]{1,0:T(8,128)S(1)}, f32[768,1024]{1,0:T(8,128)}, u32[]{:S(2)}) copy-start(f32[768,1024]{1,0:T(8,128)} %get-tuple-element.90) | copy-start | bytes 9437188
  425.8 9.6 %slice-start.4 = ((s8[6291456]{0:T(1024)(128)(4,1)}), s8[4194304]{0:T(1024)(128)(4,1)S(1)}, s32[]{:S(2)}) async-start(s8[6291456]{0:T(1024)(128)(4,1)} %bitcast.96), calls=%async_computation.4 | async-start | bytes 8388608
  431.3 4.1 slice-start.5
  433.7 7.6 %slice-start.2 = ((s8[8388608]{0:T(1024)(128)(4,1)}), s8[4194304]{0:T(1024)(128)(4,1)S(1)}, s32[]{:S(2)}) async-start(s8[8388608]{0:T(1024)(128)(4,1)} %bitcast.94), calls=%async_computation.2 | async-start | bytes 8388608
  435.4 4.6 %copy-start.11 = (f32[512,1024]{1,0:T(8,128)S(1)}, f32[512,1024]{1,0:T(8,128)}, u32[]{:S(2)}) copy-start(f32[512,1024]{1,0:T(8,128)} %get-tuple-element.96) | copy-start | bytes 6291460
  435.4 6.5 %slice-start.3 = ((s8[8388608]{0:T(1024)(128)(4,1)}), s8[4194304]{0:T(1024)(128)(4,1)S(1)}, s32[]{:S(2)}) async-start(s8[8388608]{0:T(1024)(128)(4,1)} %bitcast.94), calls=%async_computation.3 | async-start | bytes 8388608
  440.0 6.2 %slice-start = ((s8[8388608]{0:T(1024)(128)(4,1)}), s8[4194304]{0:T(1024)(128)(4,1)S(1)}, s32[]{:S(2)}) async-start(s8[8388608]{0:T(1024)(128)(4,1)} %bitcast.92), calls=%async_computation | async-start | bytes 8388608
  441.9 5.7 %slice-start.1 = ((s8[8388608]{0:T(1024)(128)(4,1)}), s8[4194304]{0:T(1024)(128)(4,1)S(1)}, s32[]{:S(2)}) async-start(s8[8388608]{0:T(1024)(128)(4,1)} %bitcast.92), calls=%async_computation.1 | async-start | bytes 8388608

commit v3 on v2

--- a/solution.py
+++ b/solution.py
@@ -17,23 +17,27 @@
 SEND = (
     "c","x","oa","ob","ja","jb","xb","ga","gb","na","fa","nb","fb","xg","cg")
 
-FETCH = 17
+FETCH = 23
 
 
 def back_kernel(shapes, R, K, delays, *refs):
     n = len(shapes)
-    (lens, up_in, down_in, part_in, mlp_in, pre_in), fetched = refs[:6], refs[6 : 6 + FETCH]
-    outs = refs[6 + FETCH : 6 + FETCH + n]
-    mlp_out, pixel_out = refs[6 + FETCH + n : 8 + FETCH + n]
-    scratch = refs[8 + FETCH + n :]
+    lens = refs[0]
+    fetched = refs[1 : 1 + FETCH]
+    outs = refs[1 + FETCH : 1 + FETCH + n]
+    ins = refs[1 + FETCH + n : 1 + FETCH + 2 * n - 1]
+    layer_out, pixel_out = refs[FETCH + 2 * n : FETCH + 2 * n + 2]
+    scratch = refs[FETCH + 2 * n + 2 :]
     held, scratch = scratch[:FETCH], scratch[FETCH:]
-    (part, normed_two, inv_two, grad_two, attended, out_w, queries, keys, values, attn_in, qkv_w,
-     normed_one, inv_one, pixel_low, pixel_hat, embed_w, gains) = held
-    (land, land_two, back_part, grad_one, one_low, zero_low, grad_att, grad_proj, grad_pix, sums,
-     out_grad, qkv_grad, embed_grad, small_grad) = scratch[:14]
-    own, cl, xl, ab, oa, ob, ja, jb, nbuf, xbl, fin, ssem, rsem, lsem, fsem, ysend, yrecv = scratch[14:]
-    ins = (up_in, down_in, out_grad, qkv_grad, embed_grad, small_grad)
+    (mlp_in, up_w, down_w, up_bias, two_low, stream_one, mean_two, inv_two, attended, out_w, queries,
+     keys, values, attn_in, qkv_w, normed_one, inv_one, pixel_low, pixel_hat, embed_w, gains, down_bias,
+     stats) = held
+    (part, mlp_part, land, land_two, grad_one, one_low, zero_low, grad_att, grad_proj, grad_pix, hidden,
+     grad_hid, sums, up_sum, down_sum, small_grad, small_total, tall, wide) = scratch[:19]
+    own, cl, xl, ab, oa, ob, ja, jb, nbuf, xbl, fin, ssem, rsem, lsem, fsem, wsem, ysend, yrecv = scratch[19:]
+    ins = (*ins[:4], small_grad, ins[4])
     slots = normed_one.shape[0] // 2
+    blocks = hidden.shape[1] // W
     H, Q, E = R//2, R//4, R//8
     i = lax.axis_index("dp"); t = lax.axis_index("tensor")
     c = lax.rem(i, 2); x = lax.rem(i//2, 2); z = i//4
@@ -47,7 +51,6 @@
     dev_j = ((3 - z)*4 + x*2 + c, t)
     dev_y = (i, 1 - t)
     fetches = [pltpu.make_async_copy(fetched[q], held[q], fsem.at[q]) for q in range(FETCH)]
-    fetches.append(pltpu.make_async_copy(pre_in, small_grad.at[pl.ds(0, 8)], fsem.at[FETCH]))
     for q in fetches:
         q.start()
     bar = pltpu.get_barrier_semaphore()
@@ -67,13 +70,19 @@
             src_ref=src, dst_ref=dst, send_sem=ysend.at[q], recv_sem=yrecv.at[q],
             device_id=dev_y, device_id_type=MESH)
 
-    first_sum = across(0, part_in, land)
-    second_sum = across(1, back_part, land_two)
-    third_sum = across(2, mlp_in, mlp_out)
-    pixel_copy = pltpu.make_async_copy(grad_pix, pixel_out, fsem.at[FETCH + 1])
-    first_sum.start()
+    def image_rows(q):
+        return pl.ds(q * slots, slots)
+
+    first_sum = [across(q, part.at[image_rows(q)], land.at[image_rows(q)]) for q in range(2)]
+    second_sum = [across(2 + q, part.at[image_rows(q)], land_two.at[image_rows(q)]) for q in range(2)]
+    third_sum = across(4, mlp_part, land)
+    pixel_copy = pltpu.make_async_copy(grad_pix, pixel_out, wsem.at[5])
+    layer_copy = pltpu.make_async_copy(one_low, layer_out, wsem.at[6])
+    total_copy = pltpu.make_async_copy(outs[4].at[pl.ds(0, 32)], small_total, wsem.at[7])
     sums[...] = jnp.zeros_like(sums)
-    small_grad[pl.ds(8, 120), :] = jnp.zeros((120, W), jnp.float32)
+    small_grad[...] = jnp.zeros_like(small_grad)
+    up_sum[...] = jnp.zeros_like(up_sum)
+    down_sum[...] = jnp.zeros_like(down_sum)
     f32, bf16 = jnp.float32, jnp.bfloat16
 
     def mm(a, b, ca, cb):
@@ -90,10 +99,65 @@
             - jnp.mean(scaled, axis=-1, keepdims=True)
             - normed * jnp.mean(scaled * normed, axis=-1, keepdims=True))
 
+    def feed(q):
+        block, rows = q // 4, pl.ds(al(lax.rem(q, 4) * 128, 128), 128)
+        cols = pl.ds(al(block * W, W), W)
+        low = two_low[rows, :]
+        up_block, down_block = up_w[:, cols], down_w[cols, :]
+        u = mm(mlp_in[rows, :], up_block, 1, 0) + up_bias[0:1, cols]
+        below = 0.5 * (1.0 + lax.erf(u * (1.0 / math.sqrt(2.0))))
+        hid = (u * below).astype(bf16)
+        slope = below + u * jnp.exp(-0.5 * u * u) * (1.0 / math.sqrt(2.0 * math.pi))
+        grad = (mm(low, down_block, 1, 1) * slope).astype(bf16)
+        hidden[rows, cols] = hid
+        grad_hid[rows, cols] = grad
+        up_sum[0:1, cols] = up_sum[0:1, cols] + jnp.sum(grad.astype(f32), axis=0, keepdims=True)
+        to_in, to_out = mm(grad, up_block, 1, 1), mm(hid, down_block, 1, 0)
+
+        @pl.when(block == 0)
+        def _():
+            part[rows, :] = to_in
+            mlp_part[rows, :] = to_out
+
+        @pl.when(block > 0)
+        def _():
+            part[rows, :] = part[rows, :] + to_in
+            mlp_part[rows, :] = mlp_part[rows, :] + to_out
+
+    def down_store(q):
+        return pltpu.make_async_copy(tall, ins[1].at[pl.ds(al(q * 256, 256), 256)], wsem.at[0])
+
+    def up_store(q):
+        rows = pl.ds(al(lax.rem(q, 2) * 512, 512), 512)
+        return pltpu.make_async_copy(wide, ins[0].at[rows, pl.ds(al((q // 2) * W, W), W)], wsem.at[1])
+
+    def out_store(q):
+        return pltpu.make_async_copy(
+            tall.at[pl.ds(0, 128)], ins[2].at[pl.ds(al(q * 128, 128), 128)], wsem.at[2])
+
+    def proj_store(q):
+        return pltpu.make_async_copy(
+            wide.at[pl.ds(0, 256)], ins[3].at[pl.ds(al(q * 256, 256), 256)], wsem.at[3])
+
+    def embed_store(q):
+        return pltpu.make_async_copy(tall, ins[5].at[pl.ds(al(q * 256, 256), 256)], wsem.at[4])
+
+    def down_weight(q):
+        tall[...] = mm(hidden[:, pl.ds(al(q * 256, 256), 256)], two_low[...], 0, 0)
+        down_store(q).start()
+
+    def up_weight(q):
+        cols = pl.ds(al(lax.rem(q, 2) * 512, 512), 512)
+        wide[...] = mm(mlp_in[:, cols], grad_hid[:, pl.ds(al((q // 2) * W, W), W)], 0, 0)
+        up_store(q).start()
+
     def second_norm(q):
         rows = pl.ds(al(q * 64, 64), 64)
-        upstream, normed = part[rows, :] + land[rows, :], normed_two[rows, :]
-        grad = grad_two[rows, :] + norm_back(upstream, normed, inv_two[rows, 0:1], gains[1:2, :])
+        upstream = part[rows, :] + land[rows, :]
+        normed = (stream_one[rows, :] - mean_two[rows, 0:1]) * inv_two[rows, 0:1]
+        low = two_low[rows, :].astype(f32)
+        down_sum[0:1, :] = down_sum[0:1, :] + jnp.sum(low, axis=0, keepdims=True)
+        grad = low + norm_back(upstream, normed, inv_two[rows, 0:1], gains[1:2, :])
         grad_one[rows, :] = grad
         one_low[rows, :] = grad.astype(bf16)
         add_sum(0, grad)
@@ -128,23 +192,25 @@
 
     def into_norm(q):
         rows = pl.ds(al(q * 128, 128), 128)
-        back_part[rows, :] = (
+        part[rows, :] = (
             mm(grad_proj[0, rows, :], qkv_w[0], 1, 1)
             + mm(grad_proj[1, rows, :], qkv_w[1], 1, 1)
             + mm(grad_proj[2, rows, :], qkv_w[2], 1, 1))
 
     def out_weight(q):
         cols = pl.ds(al(q * 128, 128), 128)
-        out_grad[cols, :] = mm(attended[:, cols], one_low[...], 0, 0)
+        tall[0:128, :] = mm(attended[:, cols], one_low[...], 0, 0)
+        out_store(q).start()
 
     def proj_weight(q):
         which, block = q // 4, lax.rem(q, 4)
         cols = pl.ds(al(block * 256, 256), 256)
-        qkv_grad[pl.ds(al(q * 256, 256), 256), :] = mm(attn_in[:, cols], grad_proj[which], 0, 0)
+        wide[0:256, :] = mm(attn_in[:, cols], grad_proj[which], 0, 0)
+        proj_store(q).start()
 
     def first_norm(q):
         rows = pl.ds(al(q * 64, 64), 64)
-        upstream, normed = back_part[rows, :] + land_two[rows, :], normed_one[rows, :]
+        upstream, normed = part[rows, :] + land_two[rows, :], normed_one[rows, :]
         grad = grad_one[rows, :] + norm_back(upstream, normed, inv_one[rows, 0:1], gains[0:1, :])
         zero_low[rows, :] = grad.astype(bf16)
         add_sum(3, upstream * normed)
@@ -153,7 +219,8 @@
 
     def embed_weight(q):
         cols = pl.ds(al(q * 256, 256), 256)
-        embed_grad[cols, :] = mm(pixel_low[:, cols], zero_low[...], 0, 0)
+        tall[...] = mm(pixel_low[:, cols], zero_low[...], 0, 0)
+        embed_store(q).start()
 
     def pixels_back(q):
         rows = pl.ds(al(q * 128, 128), 128)
@@ -163,49 +230,109 @@
         add_sum(7, grad * pixel_hat[rows, :])
 
     def pack(q):
+        for col in range(blocks):
+            small_grad[col : col + 1, :] = up_sum[0:1, col * W : (col + 1) * W]
+        for col in range(2):
+            small_grad[4 + col : 5 + col, :] = down_sum[0:1, col * W : (col + 1) * W]
         for row in range(8):
             small_grad[8 + 2 * row : 9 + 2 * row, :] = sums[row : row + 1, :W]
             small_grad[9 + 2 * row : 10 + 2 * row, :] = sums[row : row + 1, W:]
         for row, at in ((24, 0), (25, 2)):
             small_grad[row : row + 1, :] = jnp.sum(grad_proj[at].astype(f32), axis=0, keepdims=True)
 
-    def fetch_wait(q):
-        for one in fetches:
-            one.wait()
-
-    def first_wait(q):
-        first_sum.wait()
-
-    def second_start(q):
-        second_sum.start()
-
-    def second_wait(q):
-        second_sum.wait()
-        third_sum.start()
-
-    def pixel_start(q):
-        pixel_copy.start()
+    def keep_rows(q, height):
+        at = lax.rem(q, slots // height) * height + lax.broadcasted_iota(jnp.int32, (height, 1), 0)
+        return (at < lens[q // (slots // height)]).astype(f32)
+
+    def layer_end(q):
+        rows = pl.ds(al(q * 64, 64), 64)
+        total_row = stream_one[rows, :] + (mlp_part[rows, :] + land[rows, :]) + down_bias[...]
+        one_low[rows, :] = (total_row * keep_rows(q, 64)).astype(bf16)
+
+    def pixel_end(q):
+        rows = pl.ds(al(q * 128, 128), 128)
+        keep = keep_rows(q, 128)
+        first = jnp.concatenate([small_total[20:21, :], small_total[21:22, :]], axis=1)
+        cross = jnp.concatenate([small_total[22:23, :], small_total[23:24, :]], axis=1)
+        band = pixel_hat.shape[1] // 3
+        for at in range(3):
+            cols = slice(at * band, (at + 1) * band)
+            a_sum = jnp.sum(first[:, cols], axis=1, keepdims=True)
+            b_sum = jnp.sum(cross[:, cols], axis=1, keepdims=True)
+            grad_pix[rows, cols] = stats[1:2, cols] * (
+                grad_pix[rows, cols]
+                - keep * (a_sum + b_sum * pixel_hat[rows, cols]) / stats[2:3, cols])
+
+    def fetch_early(q):
+        for at in range(5):
+            fetches[at].wait()
+
+    def fetch_late(q):
+        for at in range(5, FETCH):
+            fetches[at].wait()
+
+    def act(method, *copies):
+        def piece(q):
+            for copy in copies:
+                getattr(copy, method)()
+        return piece
+
+    def landed(store):
+        return lambda q: store(q).wait()
+
+    def shift(piece, by):
+        return lambda q: piece(q + by)
+
+    def weights(begin, number, piece, store, base=0):
+        return (
+            (begin + 1, number, shift(landed(store), base)), (begin, number, shift(piece, base)))
 
     plan = (
-        (12, 1, fetch_wait), (23, 1, first_wait), (24, 8, second_norm), (32, 4, into_heads),
-        (36, 8, attention), (44, 4, into_norm), (48, 1, second_start), (49, 4, out_weight),
-        (53, 12, proj_weight), (71, 1, second_wait), (72, 8, first_norm), (80, 3, embed_weight),
-        (83, 4, pixels_back), (87, 1, pack), (88, 1, pixel_start))
-    starts, total = [], 0
-    for (rows, cols) in shapes:
-        starts.append(total); total += (rows//(2*R))*(cols//W)
+        (0, 1, fetch_early), (0, 4, feed),
+        *weights(4, 2, down_weight, down_store), *weights(4, 2, up_weight, up_store),
+        (7, 12, shift(feed, 4)), (19, 1, act("start", *first_sum)),
+        *weights(19, 2, down_weight, down_store, 2), *weights(21, 2, up_weight, up_store, 2),
+        *weights(23, 2, down_weight, down_store, 4), *weights(25, 2, up_weight, up_store, 4),
+        *weights(27, 2, down_weight, down_store, 6), *weights(29, 2, up_weight, up_store, 6),
+        (30, 1, fetch_late), (31, 1, act("wait", first_sum[0])), (31, 4, second_norm),
+        (35, 2, into_heads), (37, 4, attention), (41, 2, into_norm),
+        (42, 1, act("wait", first_sum[1])), (42, 4, shift(second_norm, 4)),
+        (43, 1, act("start", second_sum[0])),
+        (46, 2, shift(into_heads, 2)), (48, 4, shift(attention, 4)), (52, 2, shift(into_norm, 2)),
+        (54, 1, act("start", second_sum[1])),
+        (55, 1, act("wait", second_sum[0])), (55, 4, first_norm),
+        *weights(56, 4, out_weight, out_store), *weights(58, 12, proj_weight, proj_store),
+        (67, 1, act("wait", second_sum[1])), (67, 4, shift(first_norm, 4)),
+        (68, 1, act("start", third_sum)),
+        *weights(71, 3, embed_weight, embed_store), (75, 4, pixels_back), (79, 1, pack),
+        (93, 1, act("wait", third_sum)), (93, 8, layer_end), (101, 1, act("start", layer_copy)),
+        (117, 1, act("start", total_copy)), (118, 1, act("wait", total_copy)), (119, 4, pixel_end),
+        (123, 1, act("start", pixel_copy)))
+    first = 7
+    per_block = 2 * (W // (2 * R)) * 2
+    starts, total = [0, 0], 2 * per_block * blocks // 2
+    for rows_of, cols_of in shapes[2:]:
+        starts.append(total)
+        total += (rows_of // (2 * R)) * (cols_of // W)
     NC = total
+
     def slot(j): return lax.rem(j, K)
     a_mine = al(x*Q, Q); a_other = al((1-x)*Q, Q)
     e_near = al(side*E, E); e_far = al((1-side)*E, E)
     b_near = al(H + side*Q, Q); b_far = al(H + (1-side)*Q, Q)
     aN = al(x*Q + side*E, E); aF = al(x*Q + (1-side)*E, E)
     def hbm(ref, a, j, half):
-        cols = shapes[a][1]//W
-        q = j - starts[a]
-        r = al((q//cols)*(2*R) + half*R, R)
-        col = al(lax.rem(q, cols)*W, W)
-        return ref.at[pl.ds(r, R), pl.ds(col, W)]
+        if a == 0:
+            block, q = j // per_block, lax.rem(j, per_block) - per_block // 2
+            r, col = q * (2 * R) + half * R, block * W
+        elif a == 1:
+            block, q = j // per_block, lax.rem(j, per_block)
+            r, col = block * W + (q // 2) * (2 * R) + half * R, lax.rem(q, 2) * W
+        else:
+            cols = shapes[a][1] // W
+            q = j - starts[a]
+            r, col = (q // cols) * (2 * R) + half * R, lax.rem(q, cols) * W
+        return ref.at[pl.ds(al(r, R), R), pl.ds(al(col, W), W)]
     def rc(kind, src, dst, dev, s):
         k = SEND.index(kind)
         return pltpu.make_async_remote_copy(src_ref=src, dst_ref=dst, send_sem=ssem.at[k, s], recv_sem=rsem.at[k, s], device_id=dev, device_id_type=MESH)
@@ -224,23 +351,25 @@
             return rc(kind, fin.at[s, pl.ds(b_near, Q)], fin.at[s, pl.ds(b_near, Q)], dev_j if kind == "gb" else dev_o, s)
         if kind == "fb": return rc(kind, fin.at[s, pl.ds(b_far, Q)], fin.at[s, pl.ds(b_far, Q)], dev_o, s)
         if kind == "xg": return rc(kind, fin.at[s, pl.ds(a_mine, Q)], fin.at[s, pl.ds(a_mine, Q)], dev_x, s)
-        if kind == "c": return rc(kind, hbm(ins[0], 0, starts[0], 1 - c), cl.at[s], dev_c, s)
-        if kind == "cg": return rc(kind, fin.at[s], hbm(outs[0], 0, starts[0], c), dev_c, s)
+        if kind == "c": return rc(kind, ins[0].at[pl.ds(0, R), pl.ds(0, W)], cl.at[s], dev_c, s)
+        if kind == "cg": return rc(kind, fin.at[s], outs[0].at[pl.ds(0, R), pl.ds(0, W)], dev_c, s)
         raise ValueError(kind)
     def each(j, f):
         for a in range(n):
-            end = starts[a+1] if a + 1 < n else NC
-            if n == 1: f(a); continue
-            cond = (j >= starts[a]) & (j < end)
+            if a < 2:
+                late = lax.rem(j, per_block) >= per_block // 2
+                cond = (j < starts[2]) & (late if a == 0 else jnp.logical_not(late))
+            else:
+                cond = (j >= starts[a]) & (j < (starts[a + 1] if a + 1 < n else NC))
             pl.when(cond)(functools.partial(f, a))
     d = delays
     def step(tt, carry):
-        js = [tt - dd for dd in d]
+        js = [tt - first - dd for dd in d]
         def on(k): return (js[k] >= 0) & (js[k] < NC)
         @pl.when(on(7))
         def _():
             j = js[7]; s = slot(j)
-            pltpu.make_async_copy(fin.at[s], hbm(outs[0], 0, starts[0], c), lsem.at[1, s]).wait()
+            pltpu.make_async_copy(fin.at[s], outs[0].at[pl.ds(0, R), pl.ds(0, W)], lsem.at[1, s]).wait()
             desc("cg", j).wait_send(); desc("cg", j).wait_recv()
             desc("c", j).wait_send(); desc("x", j).wait_send(); desc("xg", j).wait_send()
             @pl.when(outer)
@@ -262,7 +391,7 @@
             @pl.when(inner)
             def _():
                 desc("ga", j).wait_recv(); desc("gb", j).wait_recv()
-        j5o = tt - d[5] - d[8]
+        j5o = tt - first - d[5] - d[8]
         on5o = (j5o >= 0) & (j5o < NC)
         @pl.when(on5o & outer)
         def _():
@@ -295,7 +424,7 @@
         @pl.when(on(1))
         def _():
             j = js[1]; s = slot(j)
-            pltpu.make_async_copy(hbm(ins[0], 0, starts[0], c), own.at[s], lsem.at[0, s]).wait()
+            pltpu.make_async_copy(ins[0].at[pl.ds(0, R), pl.ds(0, W)], own.at[s], lsem.at[0, s]).wait()
             desc("c", j).wait_recv()
             own[s] = own[s] + cl[s]
         @pl.when(on(6))
@@ -352,44 +481,51 @@
             else:
                 pl.when((tt >= begin) & (tt < begin + number))(functools.partial(piece, tt - begin))
         return carry
-    lax.fori_loop(0, NC + d[7], step, 0)
-    third_sum.wait()
+    lax.fori_loop(0, first + NC + d[7], step, 0)
+    layer_copy.wait()
     pixel_copy.wait()
 
 
-def back_pass(lengths, grad_up, grad_down, part, mlp_part, pre, fetched, R=64, K=14,
-              delays=(0, 1, 3, 5, 7, 9, 12, 13, 1)):
+def back_pass(lengths, fetched, R=64, K=14, delays=(0, 1, 3, 5, 7, 9, 12, 13, 1)):
     f32, bf16 = jnp.float32, jnp.bfloat16
-    tokens, width = part.shape
-    local = grad_up.shape[0] // 2
-    patch = fetched[13].shape[1]
-    shapes = (grad_up.shape, grad_down.shape, (local, width), (3 * width, local), (patch, width), (2 * R, W))
+    tokens, width = fetched[0].shape
+    hidden = fetched[1].shape[1]
+    local = fetched[8].shape[1]
+    patch = fetched[17].shape[1]
+    shapes = (
+        (width, hidden), (hidden, width), (local, width), (3 * width, local), (2 * R, W), (patch, width))
     n = len(shapes)
     H, Q, E = R // 2, R // 4, R // 8
     V = lambda r: pltpu.VMEM((K, r, W), f32)
     anywhere = pl.BlockSpec(memory_space=pl.ANY)
     held = [pltpu.VMEM(a.shape, a.dtype) for a in fetched]
     out = [jax.ShapeDtypeStruct(s, f32) for s in shapes]
-    out += [jax.ShapeDtypeStruct((tokens, width), f32), jax.ShapeDtypeStruct((tokens, patch), f32)]
-    return pl.pallas_call(
+    out += [jax.ShapeDtypeStruct(s, f32) for s in shapes[:4] + shapes[5:]]
+    out += [jax.ShapeDtypeStruct((tokens, width), bf16), jax.ShapeDtypeStruct((tokens, patch), f32)]
+    stream = pltpu.VMEM((tokens, width), f32)
+    narrow = pltpu.VMEM((tokens, width), bf16)
+    results = pl.pallas_call(
         functools.partial(back_kernel, shapes, R, K, delays),
         out_shape=out,
-        in_specs=[pl.BlockSpec(memory_space=pltpu.SMEM)] + [anywhere] * (5 + FETCH),
+        in_specs=[pl.BlockSpec(memory_space=pltpu.SMEM)] + [anywhere] * FETCH,
         out_specs=[anywhere] * len(out),
         scratch_shapes=[
             *held,
-            pltpu.VMEM((tokens, width), f32), pltpu.VMEM((tokens, width), f32), pltpu.VMEM((tokens, width), f32),
-            pltpu.VMEM((tokens, width), f32), pltpu.VMEM((tokens, width), bf16), pltpu.VMEM((tokens, width), bf16),
+            stream, stream, stream, stream, stream, narrow, narrow,
             pltpu.VMEM((tokens, local), bf16), pltpu.VMEM((3, tokens, local), bf16),
-            pltpu.VMEM((tokens, patch), f32), pltpu.VMEM((8, width), f32),
-            pltpu.VMEM(shapes[2], f32), pltpu.VMEM(shapes[3], f32), pltpu.VMEM(shapes[4], f32), pltpu.VMEM(shapes[5], f32),
+            pltpu.VMEM((tokens, patch), f32), pltpu.VMEM((tokens, hidden), bf16),
+            pltpu.VMEM((tokens, hidden), bf16), pltpu.VMEM((8, width), f32),
+            pltpu.VMEM((1, hidden), f32), pltpu.VMEM((1, width), f32), pltpu.VMEM(shapes[4], f32),
+            pltpu.VMEM((32, W), f32), pltpu.VMEM((256, width), f32), pltpu.VMEM((512, W), f32),
             V(R), V(R), V(Q), V(Q), V(Q), V(H), V(E), V(Q), V(Q), V(Q), V(R),
             pltpu.SemaphoreType.DMA((len(SEND), K)), pltpu.SemaphoreType.DMA((len(SEND), K)),
-            pltpu.SemaphoreType.DMA((2, K)), pltpu.SemaphoreType.DMA((FETCH + 2,)),
-            pltpu.SemaphoreType.DMA((3,)), pltpu.SemaphoreType.DMA((3,)),
+            pltpu.SemaphoreType.DMA((2, K)), pltpu.SemaphoreType.DMA((FETCH,)),
+            pltpu.SemaphoreType.DMA((8,)), pltpu.SemaphoreType.DMA((5,)), pltpu.SemaphoreType.DMA((5,)),
         ],
-        compiler_params=pltpu.CompilerParams(collective_id=1, has_side_effects=True, vmem_limit_bytes=66_000_000),
-        name="back_pass")(lengths, grad_up, grad_down, part, mlp_part, pre, *fetched)
+        compiler_params=pltpu.CompilerParams(
+            collective_id=1, has_side_effects=True, vmem_limit_bytes=67_000_000),
+        name="back_pass")(lengths, *fetched)
+    return (*results[:n], *results[-2:])
 
 
 def stats_kernel(ranks, band_width, lens, pix, out, mine, table, ssem, rsem):
@@ -409,7 +545,14 @@
         one = one + jnp.sum(kept, axis=0, keepdims=True)
         two = two + jnp.sum(kept * x, axis=0, keepdims=True)
         number = number + jnp.sum(keep, axis=0, keepdims=True)
-    mine[...] = jnp.concatenate([one, two, number, jnp.zeros((5, width), jnp.float32)], axis=0)
+    folded = []
+    for line in (one, two):
+        for b in range(3):
+            at = b * band_width
+            folded.append(
+                sum(line[:, at + lane : at + lane + 128] for lane in range(0, band_width, 128)))
+    folded += [number[:, :128], jnp.zeros((1, 128), jnp.float32)]
+    mine[...] = jnp.concatenate(folded, axis=0)
     pl.semaphore_wait(bar, ranks - 1)
 
     def copy(k):
@@ -436,9 +579,9 @@
         copy(k).wait_send()
     for b in range(width // band_width):
         cols = slice(b * band_width, (b + 1) * band_width)
-        count = total[2:3, cols] * float(band_width)
-        mean = jnp.sum(total[0:1, cols], axis=1, keepdims=True) / count
-        square = jnp.sum(total[1:2, cols], axis=1, keepdims=True) / count
+        count = jnp.concatenate([total[6:7, :]] * (band_width // 128), axis=1) * float(band_width)
+        mean = jnp.sum(total[b : b + 1, :], axis=1, keepdims=True) / count
+        square = jnp.sum(total[3 + b : 4 + b, :], axis=1, keepdims=True) / count
         rstd = lax.rsqrt(square - mean * mean + 1e-05)
         out[:, cols] = jnp.concatenate(
             [mean, rstd, count, jnp.zeros((5, band_width), jnp.float32)], axis=0)
@@ -452,8 +595,8 @@
         in_specs=[pl.BlockSpec(memory_space=pltpu.SMEM), pl.BlockSpec(memory_space=pltpu.VMEM)],
         out_specs=pl.BlockSpec(memory_space=pltpu.VMEM),
         scratch_shapes=[
-            pltpu.VMEM((8, width), jnp.float32),
-            pltpu.VMEM((ranks, 8, width), jnp.float32),
+            pltpu.VMEM((8, 128), jnp.float32),
+            pltpu.VMEM((ranks, 8, 128), jnp.float32),
             pltpu.SemaphoreType.DMA((ranks,)),
             pltpu.SemaphoreType.DMA((ranks,)),
         ],
@@ -607,6 +750,35 @@
     stream_one = stream_zero + attn_out + out_bias
     layer_two, normed_two, inverse_two = normalize(stream_one, norm_gain[1], norm_bias[1])
     mlp_input = layer_two.astype(jnp.bfloat16)
+    row_valid = valid_rows.reshape(tokens, 1)
+    if fast:
+        spread = lambda column: jnp.broadcast_to(column, (tokens, 128))
+        two_low = cotangent.reshape(tokens, model_width) * row_valid.astype(jnp.bfloat16)
+        mean_two = jnp.mean(stream_one, axis=-1, keepdims=True)
+        fetched = (
+            mlp_input, up_w, down_w, up_bias.reshape(1, -1), two_low, stream_one, spread(mean_two),
+            spread(inverse_two), attended, out_w, queries, key_rows, values, attn_input, qkv_w, normed_one,
+            spread(inverse_one), pixel_low, pixel_hat.reshape(tokens, patch_width), embed_w, norm_gain,
+            down_bias.reshape(1, -1), stats)
+        sum_up, sum_down, sum_out_proj, sum_qkv, small, embed_sum, output, pixel_grad = back_pass(
+            lengths, fetched)
+        rows = small[8:24].reshape(8, 2 * W)
+        return (
+            output.reshape(images, slot_count, model_width),
+            pixel_grad.reshape(images, slot_count, patch_width),
+            embed_sum,
+            rows[5],
+            jnp.stack([rows[3], rows[1]]),
+            jnp.stack([rows[4], rows[2]]),
+            sum_qkv.reshape(3, model_width, local_width),
+            small[24:26],
+            sum_out_proj,
+            rows[0],
+            sum_up,
+            small[0:4].reshape(-1),
+            sum_down,
+            small[4:6].reshape(-1),
+        )
     hidden_pre = jnp.dot(mlp_input, up_w, preferred_element_type=jnp.float32) + up_bias
     hidden_low = jax.nn.gelu(hidden_pre, approximate=False).astype(jnp.bfloat16)
     mlp_part = jnp.dot(hidden_low, down_w, preferred_element_type=jnp.float32)
@@ -620,42 +792,6 @@
     )
     grad_up = contract_rows(mlp_input, grad_hidden)
     grad_up_bias = jnp.sum(grad_hidden.astype(jnp.float32), axis=0)
-    if fast:
-        spread = lambda column: jnp.broadcast_to(column, (tokens, 128))
-        pre = jnp.concatenate([grad_up_bias, jnp.sum(grad_two, axis=0), jnp.zeros((1024,), jnp.float32)])
-        fetched = (
-            contract_cols(grad_hidden, up_w), normed_two, spread(inverse_two), grad_two, attended, out_w,
-            queries, key_rows, values, attn_input, qkv_w, normed_one, spread(inverse_one), pixel_low,
-            pixel_hat.reshape(tokens, patch_width), embed_w, norm_gain)
-        sum_up, sum_down, sum_out_proj, sum_qkv, embed_sum, small, mlp_other, grad_pixel_hat = back_pass(
-            lengths, grad_up, grad_down, fetched[0], mlp_part, pre.reshape(8, W), fetched)
-        flat = small.reshape(-1)
-        rows = small[8:24].reshape(8, 2 * W)
-        sum_up_bias, sum_down_bias = flat[:2048], flat[2048:3072]
-        band = rows[6:8, :patch_width].reshape(2, 3, band_width).sum(axis=-1)
-        stream_two = stream_one + (mlp_part + mlp_other) + down_bias
-        output = (stream_two * row_valid).astype(jnp.bfloat16).reshape(images, slot_count, model_width)
-        grad_pixel_hat = grad_pixel_hat.reshape(images, slot_count, 3, band_width)
-        pixel_grad = band_rstd[:, None] * (
-            grad_pixel_hat
-            - pixel_mask * (band[0][:, None] + band[1][:, None] * pixel_hat) / band_count
-        )
-        return (
-            output,
-            pixel_grad.reshape(images, slot_count, patch_width),
-            embed_sum,
-            rows[5],
-            jnp.stack([rows[3], rows[1]]),
-            jnp.stack([rows[4], rows[2]]),
-            sum_qkv.reshape(3, model_width, local_width),
-            small[24:26],
-            sum_out_proj,
-            rows[0],
-            sum_up,
-            sum_up_bias,
-            sum_down,
-            sum_down_bias,
-        )
     grad_mlp_in = tensor_sum(contract_cols(grad_hidden, up_w))
     grad_one = grad_two + normalize_back(grad_mlp_in, normed_two, inverse_two, norm_gain[1])
     grad_out_bias = jnp.sum(grad_one, axis=0)

time: 460 us -> 414 us (0.900); the launches traced: 451 us -> 414 us
  matrix products: 44.7 us -> 10.2 us
  other arithmetic: 25.7 us -> 19.3 us
    dot_general x6 -> x0, matrix products: 34.5 us -> none  [the longest x2 11.6 us: contract_rows(): lax.dot_general(left_side, right_side, (((0,), (0,)), ((), ())), preferre...]
    pallas_call x1, Pallas kernels: 278 us -> 286 us  [back_pass(): pl.pallas_call(functools.partial(back_kernel, shapes, R, K, delays), out_...]
    unnamed x75 -> x57, local copies, waits for them, and re-layouts: 26.9 us -> 28.4 us
where the time goes in v3:
time: 414 us
  Pallas kernels  296 us (71%)
  waiting for transfers between devices  43.1 us (10%)
  local copies, waits for them, and re-layouts  42.2 us (10%)
  other arithmetic  19.3 us (5%)
  matrix products  10.2 us (2%)
    pallas_call x1, Pallas kernels, back_pass(): pl.pallas_call(functools.partial(back_kernel, shapes, R, K, delays), out_...  286 us
    ppermute x1, waiting for transfers between devices, tensor_sum(): return part + lax.ppermute(part, 'tensor', [(0, 1), (1, 0)])  43.1 us
    unnamed x57, local copies, waits for them, and re-layouts  28.4 us
    pallas_call x1, Pallas kernels, band_stats(): pl.pallas_call(functools.partial(stats_kernel, ranks, width // 3), out_sh...  10.8 us
  transfers between devices with their start and end apart: 1, of which 1 were waited for; matrix products, arithmetic and copies ran while one was open for 1% of the time, Pallas kernels for 0%

profile of v3, /device:TPU:0, one launch (start us, length us, event | category | flops | bytes accessed | tf_op | source)
XLA Modules:
  0.0 413.7 jit_solution(13921422174727044158)
XLA Ops:
  0.7 0.7 convert_multiply_fusion
  1.3 0.7 fusion.25
  2.0 0.8 multiply_bitcast_fusion
  2.8 0.8 fusion.31
  3.6 0.8 fusion.30
  4.4 0.8 fusion.29
  5.1 10.8 %band_stats.1.refs_23_ = f32[8,768]{1,0:T(8,128)} custom-call(s32[2]{0:T(128)} %refs_0_.1, bf16[2,256,768]{2,1,0:T(8,128)(2,1)} %pix.1), custom_call_target="tpu_custom_call" | custom-call | tf_op jit(solution)/shard_map/band_stats/pallas_call | solution.py:592
  16.0 0.8 slice_reduce_fusion.1
  16.9 0.1 copy.56
  16.9 0.1 sub.46
  17.0 0.1 copy.57
  17.1 0.1 mul.132
  17.2 2.6 fusion.6
  19.8 3.7 multiply_sine_fusion.1
  23.6 1.1 fusion.32
  24.6 0.0 copy-done.4
  24.6 0.3 multiply_reduce_fusion.1
  25.0 0.0 copy-start.5
  25.0 1.8 add_convert_fusion.1
  26.8 0.9 copy-done.5
  27.7 1.5 convolution_convert_fusion.refs_12_
  29.2 1.5 fusion.8.refs_11_
  30.7 1.5 fusion.7.refs_13_
  32.3 1.6 reshape.187
  33.9 2.4 reshape.185
  36.3 2.4 reshape.186
  38.6 1.9 fusion.11
  40.6 0.0 copy-start.10
  40.6 1.5 fusion.33
  42.1 0.5 fusion.10
  42.6 0.0 copy-start.2
  42.6 0.5 copy.47
  43.2 0.1 copy.60
  43.3 0.6 copy-done.2
  43.8 2.0 fusion.34
  45.9 1.5 collective-permute-start
  47.4 1.0 copy.48.refs_9_
  48.4 2.3 bitcast_multiply_fusion.refs_5_
  50.8 43.1 %collective-permute-done = f32[512,1024]{1,0:T(8,128)} collective-permute-done((f32[512,1024]{1,0:T(8,128)}, f32[512,1024]{1,0:T(8,128)}, u32[]{:S(2)}, u32[]{:S(2)}) %collective-permute-start) | collective-permute-done | bytes 2097184 | tf_op jit(solution)/shard_map/ppermute | solution.py:657
  93.9 2.6 fusion.28
  96.5 0.3 multiply_reduce_fusion
  96.8 1.4 add_convert_fusion.refs_1_
  98.2 0.8 broadcast_in_dim.22.refs_17_
  99.1 0.8 broadcast_in_dim.21.refs_8_
  99.9 0.8 broadcast_in_dim.20.refs_7_
  100.7 285.6 %back_pass.1 = (f32[1024,2048]{1,0:T(8,128)}, f32[2048,1024]{1,0:T(8,128)}, f32[512,1024]{1,0:T(8,128)}, f32[3072,512]{1,0:T(8,128)}, f32[128,512]{1,0:T(8,128)}...) custom-call(s32[2]{0:T(128)} %refs_0_.1, ...), custom_call_target="tpu_custom_call" | custom-call | tf_op jit(solution)/shard_map/back_pass/pallas_call | solution.py:507
  386.4 0.8 slice_bitcast_fusion
  387.2 1.5 slice_bitcast_fusion.1
  388.7 0.6 copy.69
  389.3 0.6 copy.68
  389.9 0.6 copy.67
  390.5 0.6 copy.62
  391.1 0.6 pad_maximum_fusion
  391.7 2.4 copy.83
  394.2 1.1 copy.84
  395.3 1.7 copy.85
  397.0 1.7 copy-done.1
  398.7 3.2 copy.86
  401.8 0.7 copy-done.7
  402.5 1.3 copy.87
  403.9 1.1 slice-done.3
  404.9 4.2 %copy.88 = f32[1024,2048]{1,0:T(8,128)} copy(f32[1024,2048]{1,0:T(8,128)S(1)} %bitcast.83) | data formatting | bytes 16777216
  409.1 1.2 slice-done.1
  410.3 3.4 copy.89
  (44 shorter events, 0.2 us)
Async XLA Ops:
  17.2 6.3 %copy-start.8 = (bf16[768,1024]{1,0:T(8,128)(2,1)S(1)}, bf16[768,1024]{1,0:T(8,128)(2,1)}, u32[]{:S(2)}) copy-start(bf16[768,1024]{1,0:T(8,128)(2,1)} %refs_20_.1) | copy-start | bytes 4718596
  17.2 6.3 %copy-start.12 = (f32[1024]{0:T(1024)S(1)}, f32[1024]{0:T(1024)}, u32[]{:S(2)}) copy-start(f32[1024]{0:T(1024)} %param.22) | copy-start | bytes 12292
  19.8 4.8 %copy-start.4 = (bf16[512,768]{1,0:T(8,128)(2,1)}, bf16[512,768]{1,0:T(8,128)(2,1)S(1)}, u32[]{:S(2)}) copy-start(bf16[512,768]{1,0:T(8,128)(2,1)S(1)} %get-tuple-element.37.refs_18_) | copy-start | bytes 2359300
  25.0 2.7 copy-start.5
  26.8 4.0 copy-start.3
  40.6 1.5 copy-start.10
  42.6 1.2 copy-start.2
  45.9 48.0 %copy-start.11 = (f32[1024]{0:T(1024)S(1)}, f32[1024]{0:T(1024)}, u32[]{:S(2)}) copy-start(f32[1024]{0:T(1024)} %param.28) | copy-start | bytes 12292
  45.9 48.0 %collective-permute-start = (f32[512,1024]{1,0:T(8,128)}, f32[512,1024]{1,0:T(8,128)}, u32[]{:S(2)}, u32[]{:S(2)}) collective-permute-start(f32[512,1024]{1,0:T(8,128)} %fusion.34), channel_id=1, source_target_pairs={{0,1},{1,0},{2,3},{3,2},{4,5},{5,4},{6,7},{7,6},{8,9},{9,8},{10,11... | collective-permute-start | bytes 6291464 | tf_op jit(solution)/shard_map/ppermute | solution.py:657
  96.5 1.8 copy-start
  386.4 7.8 %copy-start.9 = (f32[512,768]{1,0:T(8,128)S(1)}, f32[512,768]{1,0:T(8,128)}, u32[]{:S(2)}) copy-start(f32[512,768]{1,0:T(8,128)} %get-tuple-element.23) | copy-start | bytes 4718596
  391.7 3.6 copy-start.6
  394.2 4.5 %copy-start.1 = (f32[3072,512]{1,0:T(8,128)S(1)}, f32[3072,512]{1,0:T(8,128)}, u32[]{:S(2)}) copy-start(f32[3072,512]{1,0:T(8,128)} %get-tuple-element.26) | copy-start | bytes 18874372
  395.3 8.6 %slice-start.2 = ((s8[8388608]{0:T(1024)(128)(4,1)}), s8[4194304]{0:T(1024)(128)(4,1)S(1)}, s32[]{:S(2)}) async-start(s8[8388608]{0:T(1024)(128)(4,1)} %bitcast.82), calls=%async_computation.2 | async-start | bytes 8388608
  398.6 3.9 copy-start.7
  398.7 6.3 %slice-start.3 = ((s8[8388608]{0:T(1024)(128)(4,1)}), s8[4194304]{0:T(1024)(128)(4,1)S(1)}, s32[]{:S(2)}) async-start(s8[8388608]{0:T(1024)(128)(4,1)} %bitcast.82), calls=%async_computation.3 | async-start | bytes 8388608
  402.5 6.6 %slice-start = ((s8[8388608]{0:T(1024)(128)(4,1)}), s8[4194304]{0:T(1024)(128)(4,1)S(1)}, s32[]{:S(2)}) async-start(s8[8388608]{0:T(1024)(128)(4,1)} %bitcast.80), calls=%async_computation | async-start | bytes 8388608
  404.9 5.4 %slice-start.1 = ((s8[8388608]{0:T(1024)(128)(4,1)}), s8[4194304]{0:T(1024)(128)(4,1)S(1)}, s32[]{:S(2)}) async-start(s8[8388608]{0:T(1024)(128)(4,1)} %bitcast.80), calls=%async_computation.1 | async-start | bytes 8388608

commit v4 on v3

--- a/solution.py
+++ b/solution.py
@@ -17,7 +17,7 @@
 SEND = (
     "c","x","oa","ob","ja","jb","xb","ga","gb","na","fa","nb","fb","xg","cg")
 
-FETCH = 23
+FETCH = 25
 
 
 def back_kernel(shapes, R, K, delays, *refs):
@@ -28,13 +28,14 @@
     ins = refs[1 + FETCH + n : 1 + FETCH + 2 * n - 1]
     layer_out, pixel_out = refs[FETCH + 2 * n : FETCH + 2 * n + 2]
     scratch = refs[FETCH + 2 * n + 2 :]
-    held, scratch = scratch[:FETCH], scratch[FETCH:]
-    (mlp_in, up_w, down_w, up_bias, two_low, stream_one, mean_two, inv_two, attended, out_w, queries,
-     keys, values, attn_in, qkv_w, normed_one, inv_one, pixel_low, pixel_hat, embed_w, gains, down_bias,
+    held, scratch = scratch[: FETCH - 3], scratch[FETCH - 3 :]
+    (attended, out_w, stream_one, gains, shifts, out_bias, up_w, down_w, up_bias, two_low, queries,
+     keys, values, attn_in, qkv_w, normed_one, inv_one, pixel_low, pixel_hat, embed_w, down_bias,
      stats) = held
     (part, mlp_part, land, land_two, grad_one, one_low, zero_low, grad_att, grad_proj, grad_pix, hidden,
-     grad_hid, sums, up_sum, down_sum, small_grad, small_total, tall, wide) = scratch[:19]
-    own, cl, xl, ab, oa, ob, ja, jb, nbuf, xbl, fin, ssem, rsem, lsem, fsem, wsem, ysend, yrecv = scratch[19:]
+     grad_hid, sums, up_sum, down_sum, small_grad, small_total, tall, wide, land_att, mlp_in, mean_two,
+     inv_two) = scratch[:23]
+    own, cl, xl, ab, oa, ob, ja, jb, nbuf, xbl, fin, ssem, rsem, lsem, fsem, wsem, ysend, yrecv = scratch[23:]
     ins = (*ins[:4], small_grad, ins[4])
     slots = normed_one.shape[0] // 2
     blocks = hidden.shape[1] // W
@@ -50,7 +51,15 @@
     dev_o = ((side*2 + 1 - pos)*4 + x*2 + c, t)
     dev_j = ((3 - z)*4 + x*2 + c, t)
     dev_y = (i, 1 - t)
-    fetches = [pltpu.make_async_copy(fetched[q], held[q], fsem.at[q]) for q in range(FETCH)]
+    att_wide, near_w, mate_w = fetched[FETCH - 3 :]
+    half_rows = near_w.shape[0]
+    fetches = [
+        pltpu.make_async_copy(
+            near_w, land_two.at[pl.ds(pl.multiple_of(c * half_rows, half_rows), half_rows)], fsem.at[FETCH - 2]),
+        pltpu.make_async_copy(
+            mate_w, land_two.at[pl.ds(pl.multiple_of((1 - c) * half_rows, half_rows), half_rows)],
+            fsem.at[FETCH - 1])]
+    fetches += [pltpu.make_async_copy(fetched[q], held[q], fsem.at[q]) for q in range(FETCH - 3)]
     for q in fetches:
         q.start()
     bar = pltpu.get_barrier_semaphore()
@@ -76,6 +85,10 @@
     first_sum = [across(q, part.at[image_rows(q)], land.at[image_rows(q)]) for q in range(2)]
     second_sum = [across(2 + q, part.at[image_rows(q)], land_two.at[image_rows(q)]) for q in range(2)]
     third_sum = across(4, mlp_part, land)
+    heads_sum = [
+        across(5 + q, att_wide.at[pl.ds(q * 128, 128)], land_att.at[pl.ds(q * 128, 128)]) for q in range(4)]
+    for q in heads_sum:
+        q.start()
     pixel_copy = pltpu.make_async_copy(grad_pix, pixel_out, wsem.at[5])
     layer_copy = pltpu.make_async_copy(one_low, layer_out, wsem.at[6])
     total_copy = pltpu.make_async_copy(outs[4].at[pl.ds(0, 32)], small_total, wsem.at[7])
@@ -98,6 +111,25 @@
             scaled
             - jnp.mean(scaled, axis=-1, keepdims=True)
             - normed * jnp.mean(scaled * normed, axis=-1, keepdims=True))
+
+    def project(q):
+        pl.when(q == 0)(lambda: wait_tile(0))
+        for tile in range(1, 4):
+            pl.when(q == tile)(functools.partial(wait_tile, tile))
+        rows = pl.ds(al(q * 128, 128), 128)
+        total_row = mm(attended[rows, :], out_w[...], 1, 0) + mm(
+            land_att[rows, :].astype(bf16), zero_low[...], 1, 0)
+        row = stream_one[rows, :] + total_row + out_bias[...]
+        mean = jnp.mean(row, axis=-1, keepdims=True)
+        centred = row - mean
+        inverse = lax.rsqrt(jnp.mean(centred * centred, axis=-1, keepdims=True) + 1e-06)
+        stream_one[rows, :] = row
+        mean_two[rows, :] = jnp.broadcast_to(mean, (128, 128))
+        inv_two[rows, :] = jnp.broadcast_to(inverse, (128, 128))
+        mlp_in[rows, :] = (centred * inverse * gains[1:2, :] + shifts[1:2, :]).astype(bf16)
+
+    def wait_tile(tile):
+        heads_sum[tile].wait()
 
     def feed(q):
         block, rows = q // 4, pl.ds(al(lax.rem(q, 4) * 128, 128), 128)
@@ -264,11 +296,12 @@
                 - keep * (a_sum + b_sum * pixel_hat[rows, cols]) / stats[2:3, cols])
 
     def fetch_early(q):
-        for at in range(5):
+        for at in range(12):
             fetches[at].wait()
+        zero_low[...] = land_two[...].astype(bf16)
 
     def fetch_late(q):
-        for at in range(5, FETCH):
+        for at in range(12, FETCH - 1):
             fetches[at].wait()
 
     def act(method, *copies):
@@ -288,7 +321,7 @@
             (begin + 1, number, shift(landed(store), base)), (begin, number, shift(piece, base)))
 
     plan = (
-        (0, 1, fetch_early), (0, 4, feed),
+        (0, 1, fetch_early), (0, 4, project), (0, 4, feed),
         *weights(4, 2, down_weight, down_store), *weights(4, 2, up_weight, up_store),
         (7, 12, shift(feed, 4)), (19, 1, act("start", *first_sum)),
         *weights(19, 2, down_weight, down_store, 2), *weights(21, 2, up_weight, up_store, 2),
@@ -488,9 +521,9 @@
 
 def back_pass(lengths, fetched, R=64, K=14, delays=(0, 1, 3, 5, 7, 9, 12, 13, 1)):
     f32, bf16 = jnp.float32, jnp.bfloat16
-    tokens, width = fetched[0].shape
-    hidden = fetched[1].shape[1]
-    local = fetched[8].shape[1]
+    tokens, width = fetched[2].shape
+    hidden = fetched[6].shape[1]
+    local = fetched[0].shape[1]
     patch = fetched[17].shape[1]
     shapes = (
         (width, hidden), (hidden, width), (local, width), (3 * width, local), (2 * R, W), (patch, width))
@@ -498,7 +531,7 @@
     H, Q, E = R // 2, R // 4, R // 8
     V = lambda r: pltpu.VMEM((K, r, W), f32)
     anywhere = pl.BlockSpec(memory_space=pl.ANY)
-    held = [pltpu.VMEM(a.shape, a.dtype) for a in fetched]
+    held = [pltpu.VMEM(a.shape, a.dtype) for a in fetched[:-3]]
     out = [jax.ShapeDtypeStruct(s, f32) for s in shapes]
     out += [jax.ShapeDtypeStruct(s, f32) for s in shapes[:4] + shapes[5:]]
     out += [jax.ShapeDtypeStruct((tokens, width), bf16), jax.ShapeDtypeStruct((tokens, patch), f32)]
@@ -517,10 +550,11 @@
             pltpu.VMEM((tokens, hidden), bf16), pltpu.VMEM((8, width), f32),
             pltpu.VMEM((1, hidden), f32), pltpu.VMEM((1, width), f32), pltpu.VMEM(shapes[4], f32),
             pltpu.VMEM((32, W), f32), pltpu.VMEM((256, width), f32), pltpu.VMEM((512, W), f32),
+            pltpu.VMEM((tokens, local), f32), narrow, pltpu.VMEM((tokens, 128), f32), pltpu.VMEM((tokens, 128), f32),
             V(R), V(R), V(Q), V(Q), V(Q), V(H), V(E), V(Q), V(Q), V(Q), V(R),
             pltpu.SemaphoreType.DMA((len(SEND), K)), pltpu.SemaphoreType.DMA((len(SEND), K)),
             pltpu.SemaphoreType.DMA((2, K)), pltpu.SemaphoreType.DMA((FETCH,)),
-            pltpu.SemaphoreType.DMA((8,)), pltpu.SemaphoreType.DMA((5,)), pltpu.SemaphoreType.DMA((5,)),
+            pltpu.SemaphoreType.DMA((8,)), pltpu.SemaphoreType.DMA((9,)), pltpu.SemaphoreType.DMA((9,)),
         ],
         compiler_params=pltpu.CompilerParams(
             collective_id=1, has_side_effects=True, vmem_limit_bytes=67_000_000),
@@ -602,6 +636,53 @@
         ],
         compiler_params=pltpu.CompilerParams(collective_id=2, has_side_effects=True),
         name="band_stats")(lengths, pixels)
+
+
+def heads_kernel(lens, attn_in, qkv_w, bias, queries, keys, values, attended, wide):
+    f32, bf16 = jnp.float32, jnp.bfloat16
+    slots = attn_in.shape[0] // lens.shape[0]
+
+    def mm(a, b, ca, cb):
+        return lax.dot_general(a, b, (((ca,), (cb,)), ((), ())), preferred_element_type=f32)
+
+    queries[...] = (mm(attn_in[...], qkv_w[0], 1, 0) + bias[0:1, :]).astype(bf16)
+    keys[...] = mm(attn_in[...], qkv_w[1], 1, 0).astype(bf16)
+    values[...] = (mm(attn_in[...], qkv_w[2], 1, 0) + bias[1:2, :]).astype(bf16)
+    pairs = queries.shape[1] // 128
+
+    def piece(q, carry):
+        image, pair = q // pairs, lax.rem(q, pairs)
+        rows = pl.ds(pl.multiple_of(image * slots, slots), slots)
+        cols = pl.ds(pl.multiple_of(pair * 128, 128), 128)
+        qs, ks, vs = queries[rows, cols], keys[rows, cols], values[rows, cols]
+        keep = lax.broadcasted_iota(jnp.int32, (1, slots), 1) < lens[image]
+        heads = []
+        for h in range(2):
+            at = slice(h * HD, (h + 1) * HD)
+            scores = mm(qs[:, at], ks[:, at], 1, 1) * (1.0 / math.sqrt(HD))
+            scores = jnp.where(keep, scores, -1e30)
+            exps = jnp.exp(scores - jnp.max(scores, axis=-1, keepdims=True))
+            probs = exps / jnp.sum(exps, axis=-1, keepdims=True)
+            heads.append(mm(probs.astype(bf16), vs[:, at], 1, 0))
+        joined = jnp.concatenate(heads, axis=1).astype(bf16)
+        attended[rows, cols] = joined
+        wide[rows, cols] = joined.astype(f32)
+        return carry
+
+    lax.fori_loop(0, lens.shape[0] * pairs, piece, 0)
+
+
+def heads_forward(lengths, attn_in, qkv_w, bias):
+    tokens, local = attn_in.shape[0], qkv_w.shape[2]
+    vmem = pl.BlockSpec(memory_space=pltpu.VMEM)
+    low = jax.ShapeDtypeStruct((tokens, local), jnp.bfloat16)
+    return pl.pallas_call(
+        heads_kernel,
+        out_shape=[low, low, low, low, jax.ShapeDtypeStruct((tokens, local), jnp.float32)],
+        in_specs=[pl.BlockSpec(memory_space=pltpu.SMEM), vmem, vmem, vmem],
+        out_specs=[vmem] * 5,
+        compiler_params=pltpu.CompilerParams(vmem_limit_bytes=32 << 20),
+        name="heads_forward")(lengths, attn_in, qkv_w, bias)
 
 
 def positions(patch_ids, gsd_values, model_width, grid_side):
@@ -690,6 +771,11 @@
     pixel_grid = pixels.astype(jnp.float32).reshape(images, slot_count, 3, band_width)
     pixel_mask = valid_rows[:, :, None, None]
     if fast:
+        half = local_width // 2
+        core = lax.rem(lax.axis_index("dp"), 2)
+        near_w = lax.dynamic_slice_in_dim(out_w, core * half, half, 0).astype(jnp.float32)
+        near_w = lax.ppermute(near_w, "tensor", [(0, 1), (1, 0)])
+        mate_w = lax.ppermute(near_w, "dp", [(k, k ^ 1) for k in range(16)])
         stats = band_stats(pixels, lengths, 16)
         band_mean = stats[0].reshape(3, band_width)[:, 0]
         band_rstd = stats[1].reshape(3, band_width)[:, 0]
@@ -713,53 +799,16 @@
     )
     layer_one, normed_one, inverse_one = normalize(stream_zero, norm_gain[0], norm_bias[0])
     attn_input = layer_one.astype(jnp.bfloat16)
-    queries = (
-        jnp.dot(attn_input, qkv_w[0], preferred_element_type=jnp.float32) + qv_bias[0]
-    ).astype(jnp.bfloat16)
-    key_rows = jnp.dot(attn_input, qkv_w[1], preferred_element_type=jnp.float32).astype(
-        jnp.bfloat16
-    )
-    values = (
-        jnp.dot(attn_input, qkv_w[2], preferred_element_type=jnp.float32) + qv_bias[1]
-    ).astype(jnp.bfloat16)
-    query_heads = queries.reshape(images, slot_count, heads_here, head_dim)
-    key_heads = key_rows.reshape(images, slot_count, heads_here, head_dim)
-    value_heads = values.reshape(images, slot_count, heads_here, head_dim)
-
-    def score_block():
-        scores = (
-            jnp.einsum(
-                "ichd,ijhd->ihcj", query_heads, key_heads, preferred_element_type=jnp.float32
-            )
-            * score_scale
-        )
-        return jnp.where(key_keep[:, None, None, :], scores, -1e30)
-
-    scores = score_block()
-    top_score = jnp.max(scores, axis=-1, keepdims=True)
-    exp_scores = jnp.exp(scores - top_score)
-    exp_total = jnp.sum(exp_scores, axis=-1, keepdims=True)
-    log_total = top_score + jnp.log(exp_total)
-    prob_low = (exp_scores / exp_total).astype(jnp.bfloat16)
-    attended = (
-        jnp.einsum("ihcj,ijhd->ichd", prob_low, value_heads, preferred_element_type=jnp.float32)
-        .astype(jnp.bfloat16)
-        .reshape(tokens, local_width)
-    )
-    attn_out = tensor_sum(jnp.dot(attended, out_w, preferred_element_type=jnp.float32))
-    stream_one = stream_zero + attn_out + out_bias
-    layer_two, normed_two, inverse_two = normalize(stream_one, norm_gain[1], norm_bias[1])
-    mlp_input = layer_two.astype(jnp.bfloat16)
-    row_valid = valid_rows.reshape(tokens, 1)
     if fast:
+        row_valid = valid_rows.reshape(tokens, 1)
+        queries, key_rows, values, attended, att_wide = heads_forward(lengths, attn_input, qkv_w, qv_bias)
         spread = lambda column: jnp.broadcast_to(column, (tokens, 128))
         two_low = cotangent.reshape(tokens, model_width) * row_valid.astype(jnp.bfloat16)
-        mean_two = jnp.mean(stream_one, axis=-1, keepdims=True)
         fetched = (
-            mlp_input, up_w, down_w, up_bias.reshape(1, -1), two_low, stream_one, spread(mean_two),
-            spread(inverse_two), attended, out_w, queries, key_rows, values, attn_input, qkv_w, normed_one,
-            spread(inverse_one), pixel_low, pixel_hat.reshape(tokens, patch_width), embed_w, norm_gain,
-            down_bias.reshape(1, -1), stats)
+            attended, out_w, stream_zero, norm_gain, norm_bias, out_bias.reshape(1, -1), up_w, down_w,
+            up_bias.reshape(1, -1), two_low, queries, key_rows, values, attn_input, qkv_w, normed_one,
+            spread(inverse_one), pixel_low, pixel_hat.reshape(tokens, patch_width), embed_w,
+            down_bias.reshape(1, -1), stats, att_wide, near_w, mate_w)
         sum_up, sum_down, sum_out_proj, sum_qkv, small, embed_sum, output, pixel_grad = back_pass(
             lengths, fetched)
         rows = small[8:24].reshape(8, 2 * W)
@@ -779,6 +828,43 @@
             sum_down,
             small[4:6].reshape(-1),
         )
+    queries = (
+        jnp.dot(attn_input, qkv_w[0], preferred_element_type=jnp.float32) + qv_bias[0]
+    ).astype(jnp.bfloat16)
+    key_rows = jnp.dot(attn_input, qkv_w[1], preferred_element_type=jnp.float32).astype(
+        jnp.bfloat16
+    )
+    values = (
+        jnp.dot(attn_input, qkv_w[2], preferred_element_type=jnp.float32) + qv_bias[1]
+    ).astype(jnp.bfloat16)
+    query_heads = queries.reshape(images, slot_count, heads_here, head_dim)
+    key_heads = key_rows.reshape(images, slot_count, heads_here, head_dim)
+    value_heads = values.reshape(images, slot_count, heads_here, head_dim)
+
+    def score_block():
+        scores = (
+            jnp.einsum(
+                "ichd,ijhd->ihcj", query_heads, key_heads, preferred_element_type=jnp.float32
+            )
+            * score_scale
+        )
+        return jnp.where(key_keep[:, None, None, :], scores, -1e30)
+
+    scores = score_block()
+    top_score = jnp.max(scores, axis=-1, keepdims=True)
+    exp_scores = jnp.exp(scores - top_score)
+    exp_total = jnp.sum(exp_scores, axis=-1, keepdims=True)
+    log_total = top_score + jnp.log(exp_total)
+    prob_low = (exp_scores / exp_total).astype(jnp.bfloat16)
+    attended = (
+        jnp.einsum("ihcj,ijhd->ichd", prob_low, value_heads, preferred_element_type=jnp.float32)
+        .astype(jnp.bfloat16)
+        .reshape(tokens, local_width)
+    )
+    attn_out = tensor_sum(jnp.dot(attended, out_w, preferred_element_type=jnp.float32))
+    stream_one = stream_zero + attn_out + out_bias
+    layer_two, normed_two, inverse_two = normalize(stream_one, norm_gain[1], norm_bias[1])
+    mlp_input = layer_two.astype(jnp.bfloat16)
     hidden_pre = jnp.dot(mlp_input, up_w, preferred_element_type=jnp.float32) + up_bias
     hidden_low = jax.nn.gelu(hidden_pre, approximate=False).astype(jnp.bfloat16)
     mlp_part = jnp.dot(hidden_low, down_w, preferred_element_type=jnp.float32)

time: 414 us -> 381 us (0.920)
  waiting for transfers between devices: 43.1 us -> 2.54 us
  Pallas kernels: 296 us -> 323 us
  matrix products: 10.2 us -> 1.09 us
  local copies, waits for them, and re-layouts: 42.2 us -> 35.4 us
  other arithmetic: 19.3 us -> 14.4 us
    ppermute x1 -> x2, waiting for transfers between devices: 43.1 us -> 2.54 us  [the longest x1 2.54 us: per_device(): near_w = lax.ppermute(near_w, 'tensor', [(0, 1), (1, 0)])]
    pallas_call x1, Pallas kernels: 286 us -> 304 us  [back_pass(): pl.pallas_call(functools.partial(back_kernel, shapes, R, K, delays), out_...]
    pallas_call x0 -> x1, Pallas kernels: none -> 10.2 us  [heads_forward(): pl.pallas_call(heads_kernel, out_shape=[low, low, low, low, jax.ShapeDtyp...]
    dot_general x6 -> x0, matrix products: 9.1 us -> none  [the longest x1 2.04 us: per_device(): jnp.dot(attended, out_w, preferred_element_type=jnp.float32)]
    reshape x4 -> x0, local copies, waits for them, and re-layouts: 7.39 us -> none  [the longest x1 2.37 us: per_device(): value_heads = values.reshape(images, slot_count, heads_here, head_dim)]
    unnamed x57 -> x82, local copies, waits for them, and re-layouts: 28.4 us -> 33.6 us
  transfers between devices with their start and end apart: 1 -> 2, of which waited for: 1 -> 1; matrix products, arithmetic and copies ran while one was open for 1% -> 4% of each run, Pallas kernels for 0% -> 5%
where the time goes in v4:
time: 381 us
  Pallas kernels  323 us (85%)
  local copies, waits for them, and re-layouts  35.4 us (9%)
  other arithmetic  14.4 us (4%)
    pallas_call x1, Pallas kernels, back_pass(): pl.pallas_call(functools.partial(back_kernel, shapes, R, K, delays), out_...  304 us
    unnamed x82, local copies, waits for them, and re-layouts  33.6 us
    pallas_call x1, Pallas kernels, heads_forward(): pl.pallas_call(heads_kernel, out_shape=[low, low, low, low, jax.ShapeDtyp...  10.2 us
    pallas_call x1, Pallas kernels, band_stats(): pl.pallas_call(functools.partial(stats_kernel, ranks, width // 3), out_sh...  9.45 us
  transfers between devices with their start and end apart: 2, of which 1 were waited for; matrix products, arithmetic and copies ran while one was open for 4% of the time, Pallas kernels for 5%

profile of v4, /device:TPU:0, one launch (start us, length us, event | category | flops | bytes accessed | tf_op | source)
XLA Modules:
  0.0 380.7 jit_solution(14429301038221860103)
XLA Ops:
  0.6 0.0 copy-start.7
  0.7 0.0 copy-start.14
  0.7 2.2 dynamic-slice_convert_fusion
  2.9 3.0 collective-permute-start
  5.9 0.7 convert_multiply_fusion
  6.6 0.8 multiply_bitcast_fusion
  7.3 5.4 %multiply_sine_fusion.1 = (f32[512,256]{1,0:T(8,128)}, f32[512,256]{1,0:T(8,128)}, f32[512,256]{1,0:T(8,128)}, f32[512,256]{1,0:T(8,128)}) fusion(f32[256]{0:T(256)S(1)} %multiply_exponential_fusion, f32[512]{0:T(512)S(1)} %bitcast.71, f32[512]{0:T(512)S(1)} %bitcast.72), kind=kLoop, calls=%fused_computation.10 | loop fusion | flops 262144 | bytes 2102272 | tf_op jit(solution)/shard_map/sin | solution.py:697
  12.7 0.0 copy-done.7
  12.7 0.1 fusion.6
  12.8 9.4 %band_stats.1.refs_22_ = f32[8,768]{1,0:T(8,128)} custom-call(s32[2]{0:T(128)} %refs_0_.1, bf16[2,256,768]{2,1,0:T(8,128)(2,1)} %pix.1), custom_call_target="tpu_custom_call" | custom-call | tf_op jit(solution)/shard_map/band_stats/pallas_call | solution.py:626
  22.2 0.8 slice_reduce_fusion.1
  23.1 0.1 copy.33
  23.2 0.1 sub.30
  23.3 0.1 copy.34
  23.4 0.1 mul.108
  23.5 0.0 copy-start.24
  23.5 1.4 fusion
  24.9 0.4 copy-done.23
  25.3 0.3 copy-done.24
  25.6 1.1 fusion.7
  26.7 0.0 copy-start.10
  26.7 0.0 slice-start.4
  26.7 0.0 slice-start.5
  26.7 2.5 collective-permute-done.refs_24_
  29.2 0.0 collective-permute-start.1
  29.2 0.3 multiply_reduce_fusion
  29.6 0.0 slice-done.5
  29.6 0.0 copy-start
  29.6 0.0 copy-start.8
  29.6 0.0 copy-start.9
  29.7 1.8 add_convert_fusion
  31.4 0.0 copy-done.18
  31.4 0.8 copy-done
  32.3 0.0 copy-done.8
  32.3 10.2 %heads_forward.1 = (bf16[512,512]{1,0:T(8,128)(2,1)S(1)}, bf16[512,512]{1,0:T(8,128)(2,1)S(1)}, bf16[512,512]{1,0:T(8,128)(2,1)S(1)}, bf16[512,512]{1,0:T(8,128)(2,1)S(1)}, f32[512,512]{1,0:T(8,128)S(1)}) custom-call(s32[2]{0:T(128)S(1)} %copy-done.8, bf16[512,1024]{1,0:T(8,128)(2,1)S(1)} %get-tuple-element.42.attn_in.refs_14_, ...), custom_call_target="tpu_custom_call" | custom-call | tf_op jit(solution)/shard_map/heads_forward/pallas_call | solution.py:679
  42.5 0.0 copy-start.2
  42.5 1.0 copy-done.2
  43.5 0.8 copy-done.3
  44.3 0.8 copy-done.4
  45.1 0.8 copy-done.5
  45.9 0.8 copy-done.6
  46.7 1.2 bitcast_multiply_fusion.refs_10_
  47.9 0.0 collective-permute-done.1.refs_25_
  47.9 1.0 copy-done.19
  48.8 0.8 broadcast_in_dim.2.refs_17_
  49.7 303.7 %back_pass.1 = (f32[1024,2048]{1,0:T(8,128)}, f32[2048,1024]{1,0:T(8,128)}, f32[512,1024]{1,0:T(8,128)}, f32[3072,512]{1,0:T(8,128)}, f32[128,512]{1,0:T(8,128)}...) custom-call(s32[2]{0:T(128)} %refs_0_.1, ...), custom_call_target="tpu_custom_call" | custom-call | tf_op jit(solution)/shard_map/back_pass/pallas_call | solution.py:540
  353.4 0.8 slice_bitcast_fusion
  354.2 1.5 slice_bitcast_fusion.1
  355.7 0.6 copy.45
  356.3 0.6 copy.44
  356.9 0.6 copy.43
  357.5 0.6 copy.38
  358.1 0.6 pad_maximum_fusion
  358.7 2.4 copy.53
  361.1 1.1 copy.54
  362.3 1.7 copy.55
  363.9 1.7 copy-done.11
  365.6 3.2 copy.56
  368.8 0.7 copy-done.15
  369.5 1.3 copy.57
  370.8 1.1 slice-done.3
  371.9 4.2 %copy.58 = f32[1024,2048]{1,0:T(8,128)} copy(f32[1024,2048]{1,0:T(8,128)S(1)} %bitcast.59) | data formatting | bytes 16777216
  376.1 1.2 slice-done.1
  377.3 3.4 copy.59
  (55 shorter events, 0.2 us)
Async XLA Ops:
  0.6 12.0 %copy-start.7 = (s32[2]{0:T(128)S(1)}, s32[2]{0:T(128)}, u32[]{:S(2)}) copy-start(s32[2]{0:T(128)} %refs_0_.1) | copy-start | bytes 28
  0.7 22.8 %copy-start.14 = (bf16[2,256,768]{2,1,0:T(8,128)(2,1)S(1)}, bf16[2,256,768]{2,1,0:T(8,128)(2,1)}, u32[]{:S(2)}) copy-start(bf16[2,256,768]{2,1,0:T(8,128)(2,1)} %pix.1) | copy-start | bytes 2359300
  2.9 26.4 %collective-permute-start = (f32[256,1024]{1,0:T(8,128)}, f32[256,1024]{1,0:T(8,128)S(1)}, u32[]{:S(2)}, u32[]{:S(2)}) collective-permute-start(f32[256,1024]{1,0:T(8,128)} %dynamic-slice_convert_fusion), channel_id=1, source_target_pairs={{0,1},{1,0},{2,3},{3,2},{4,5},{5,4},{6,7},{7,6},{8,9},{9,8},{10,11... | collective-permute-start | bytes 3145736 | tf_op jit(solution)/shard_map/ppermute | solution.py:777
  12.7 12.2 %copy-start.16 = (bf16[768,1024]{1,0:T(8,128)(2,1)S(1)}, bf16[768,1024]{1,0:T(8,128)(2,1)}, u32[]{:S(2)}) copy-start(bf16[768,1024]{1,0:T(8,128)(2,1)} %refs_20_.1) | copy-start | bytes 4718596
  12.7 12.2 %copy-start.25 = (f32[1024]{0:T(1024)S(1)}, f32[1024]{0:T(1024)}, u32[]{:S(2)}) copy-start(f32[1024]{0:T(1024)} %param.22) | copy-start | bytes 12292
  23.5 1.4 copy-start.21
  23.5 1.4 copy-start.22
  23.5 1.8 copy-start.23
  23.5 2.1 copy-start.24
  24.9 1.8 copy-start.12
  26.7 4.8 %copy-start.10 = (f32[512,1024]{1,0:T(8,128)}, f32[512,1024]{1,0:T(8,128)S(1)}, u32[]{:S(2)}) copy-start(f32[512,1024]{1,0:T(8,128)S(1)} %get-tuple-element.63.refs_3_) | copy-start | bytes 6291460
  26.7 2.9 slice-start.4
  26.7 2.9 slice-start.5
  29.2 2.2 copy-start.18
  29.2 18.6 %collective-permute-start.1 = (f32[256,1024]{1,0:T(8,128)S(1)}, f32[256,1024]{1,0:T(8,128)S(1)}, u32[]{:S(2)}, u32[]{:S(2)}) collective-permute-start(f32[256,1024]{1,0:T(8,128)S(1)} %collective-permute-done.refs_24_), channel_id=1, source_target_pairs={{0,2},{2,0},{4,6},{6,4},{8,10},{10,8},{12,14},{14,12},{16,18},{18,... | collective-permute-start | bytes 3145736 | tf_op jit(solution)/shard_map/ppermute | solution.py:778
  29.6 2.6 copy-start
  29.6 2.6 copy-start.8
  29.6 2.6 copy-start.9
  31.4 11.1 %copy-start.1 = (bf16[512,1024]{1,0:T(8,128)(2,1)}, bf16[512,1024]{1,0:T(8,128)(2,1)S(1)}, u32[]{:S(2)}) copy-start(bf16[512,1024]{1,0:T(8,128)(2,1)S(1)} %get-tuple-element.42.attn_in.refs_14_) | copy-start | bytes 3145732
  32.3 14.4 %copy-start.20 = (bf16[2,256,1024]{2,1,0:T(8,128)(2,1)S(1)}, bf16[2,256,1024]{2,1,0:T(8,128)(2,1)}, u32[]{:S(2)}) copy-start(bf16[2,256,1024]{2,1,0:T(8,128)(2,1)} %param.33) | copy-start | bytes 3145732
  42.5 1.0 copy-start.2
  43.5 0.8 copy-start.3
  44.3 0.8 copy-start.4
  45.1 0.8 copy-start.5
  45.9 0.8 copy-start.6
  47.9 1.0 copy-start.19
  353.4 7.8 %copy-start.17 = (f32[512,768]{1,0:T(8,128)S(1)}, f32[512,768]{1,0:T(8,128)}, u32[]{:S(2)}) copy-start(f32[512,768]{1,0:T(8,128)} %get-tuple-element.33) | copy-start | bytes 4718596
  358.7 3.6 copy-start.13
  361.1 4.5 %copy-start.11 = (f32[3072,512]{1,0:T(8,128)S(1)}, f32[3072,512]{1,0:T(8,128)}, u32[]{:S(2)}) copy-start(f32[3072,512]{1,0:T(8,128)} %get-tuple-element.36) | copy-start | bytes 18874372
  362.3 8.6 %slice-start.2 = ((s8[8388608]{0:T(1024)(128)(4,1)}), s8[4194304]{0:T(1024)(128)(4,1)S(1)}, s32[]{:S(2)}) async-start(s8[8388608]{0:T(1024)(128)(4,1)} %bitcast.58), calls=%async_computation.2 | async-start | bytes 8388608
  365.6 3.9 %copy-start.15 = (f32[512,1024]{1,0:T(8,128)S(1)}, f32[512,1024]{1,0:T(8,128)}, u32[]{:S(2)}) copy-start(f32[512,1024]{1,0:T(8,128)} %get-tuple-element.88) | copy-start | bytes 6291460
  365.6 6.3 %slice-start.3 = ((s8[8388608]{0:T(1024)(128)(4,1)}), s8[4194304]{0:T(1024)(128)(4,1)S(1)}, s32[]{:S(2)}) async-start(s8[8388608]{0:T(1024)(128)(4,1)} %bitcast.58), calls=%async_computation.3 | async-start | bytes 8388608
  369.5 6.6 %slice-start = ((s8[8388608]{0:T(1024)(128)(4,1)}), s8[4194304]{0:T(1024)(128)(4,1)S(1)}, s32[]{:S(2)}) async-start(s8[8388608]{0:T(1024)(128)(4,1)} %bitcast.56), calls=%async_computation | async-start | bytes 8388608
  371.9 5.4 %slice-start.1 = ((s8[8388608]{0:T(1024)(128)(4,1)}), s8[4194304]{0:T(1024)(128)(4,1)S(1)}, s32[]{:S(2)}) async-start(s8[8388608]{0:T(1024)(128)(4,1)} %bitcast.56), calls=%async_computation.1 | async-start | bytes 8388608
